TPU v7x, 32 devices: a whole 2x2x4 slice. The times are simulated.
32 devices in a mesh: dom: 16 (over z, y, x), tp: 2 (over core).
Axes of the slice: x: 2, y: 2, z: 4, core: 2. Of those that a mesh axis runs over, the one named last changes fastest.
Arguments:
- node_latent: bfloat16 [16384, 128], P('dom'), may hold values from -6 to 6
- edge_latent: bfloat16 [131072, 128], P(('dom', 'tp')), may hold values from -6 to 6
- edge_sender: int32 [131072], P(('dom', 'tp')), may hold values from 0 to 1535, as said below
- edge_receiver: int32 [131072], P(('dom', 'tp')), may hold values from 0 to 1535, as said below
- edge_count: int32 [32], P(('dom', 'tp')), may hold values from 2048 to 4096, as said below
- send_index: int32 [16, 4, 128], P('dom'), may hold values from -1 to 1023, as said below
- edge_in: bfloat16 [3, 384, 128], P(None, None, 'tp'), may hold values from -0.3125 to 0.3125
- edge_out: bfloat16 [3, 128, 128], P(None, 'tp'), may hold values from -0.5 to 0.5
- node_in: bfloat16 [3, 256, 128], P(None, None, 'tp'), may hold values from -0.375 to 0.375
- node_out: bfloat16 [3, 128, 128], P(None, 'tp'), may hold values from -0.5 to 0.5
Outputs:
- node_result: bfloat16 [16384, 128], P('dom')
- edge_result: bfloat16 [131072, 128], P(('dom', 'tp'))
Inputs may be any that keep to these rules, and one draw needn't show every extreme that they name: `send_index`: entry [p, k, j] is a local node index of partition p sent to partition (p + o_k) mod 16, with o = (1, -1, 2, -2); -1 marks padding, which stands only after the live entries of a block; live entries of a block are distinct; at least half of each block is live and some block is full. `edge_sender`: an index below 1024 is an owned node of the slot's partition; index 1024 + k * 128 + j is slot j of halo block k; never a padding halo slot. `edge_receiver`: as for edge_sender. `edge_count`: some device block is full.
All inputs are finite; a program needn't handle non-finite values.
Results may differ from a plain program's by a relative error of at most 0.013.
Values may be sent and summed in bfloat16 or wider, within the bound.
A program may use at most 64 MiB of HBM per device.

v0:
```python
import jax
import jax.numpy as jnp
from jax import lax
from jax.sharding import PartitionSpec as P

LAYERS = 3


neighbour_offsets = (1, -1, 2, -2)
norm_floor = 0.25


def from_behind(array, axis, by):
    length = lax.axis_size(axis)
    return lax.ppermute(array, axis, [(i, (i + by) % length) for i in range(length)])


def layer_norm(values):
    centre = jnp.mean(values, axis=-1, keepdims=True)
    centred = values - centre
    spread = jnp.mean(centred * centred, axis=-1, keepdims=True)
    return centred * lax.rsqrt(spread + norm_floor)


def product(first_operand, second_operand):
    return jnp.dot(first_operand, second_operand, preferred_element_type=jnp.float32)


def column_sum(table, values, exact):
    if exact:
        return lax.dot_general(
            table,
            values,
            (((0,), (0,)), ((), ())),
            precision=lax.Precision.HIGHEST,
            preferred_element_type=jnp.float32,
        )
    return lax.dot_general(
        table, values, (((0,), (0,)), ((), ())), preferred_element_type=jnp.float32
    )


def fetch_halo(nodes_now, pick_table):
    feature_width = nodes_now.shape[1]
    picked = (
        product(pick_table, nodes_now)
        .astype(jnp.bfloat16)
        .reshape(len(neighbour_offsets), -1, feature_width)
    )
    blocks = [
        from_behind(picked[neighbour], "dom", offset)
        for neighbour, offset in enumerate(neighbour_offsets)
    ]
    return jnp.concatenate(blocks, axis=0)


def return_sums(returned, pick_float, owned_sums):
    arrived = [
        from_behind(returned[neighbour].astype(jnp.bfloat16), "dom", -offset).astype(jnp.float32)
        for neighbour, offset in enumerate(neighbour_offsets)
    ]
    return owned_sums + column_sum(pick_float, jnp.concatenate(arrived, axis=0), True)


def local(
    node_latent,
    edge_latent,
    edge_sender,
    edge_receiver,
    edge_count,
    send_index,
    edge_in,
    edge_out,
    node_in,
    node_out,
):
    feature_width = node_latent.shape[1]
    node_total = node_latent.shape[0]
    share_rows = node_total // lax.axis_size("tp")
    first_row = lax.axis_index("tp") * share_rows
    edge_rows = edge_latent.shape[0]
    block_rows = min(512, edge_rows)
    block_count = edge_rows // block_rows
    flat_index = send_index[0].reshape(-1)
    halo_total = flat_index.shape[0]
    extended_total = node_total + halo_total
    pick_match = flat_index[:, None] == jnp.arange(node_total, dtype=jnp.int32)[None, :]
    pick_table = pick_match.astype(jnp.bfloat16)
    pick_float = pick_match.astype(jnp.float32)
    live_edges = jnp.arange(edge_rows, dtype=jnp.int32) < edge_count[0]
    sender_blocks = edge_sender.reshape(block_count, block_rows)
    receiver_blocks = edge_receiver.reshape(block_count, block_rows)
    live_blocks = live_edges.reshape(block_count, block_rows)
    extended_columns = jnp.arange(extended_total, dtype=jnp.int32)
    full_in, full_out = (
        lax.all_gather(edge_in, "tp", axis=2, tiled=True),
        lax.all_gather(edge_out, "tp", axis=1, tiled=True),
    )
    node_first, node_second = (
        lax.all_gather(node_in, "tp", axis=2, tiled=True),
        lax.all_gather(node_out, "tp", axis=1, tiled=True),
    )
    nodes_now = node_latent
    edges_now = edge_latent
    for layer_index in range(LAYERS):
        halo_rows = fetch_halo(nodes_now, pick_table)
        extended = jnp.concatenate([nodes_now, halo_rows], axis=0)
        weight_in = full_in[layer_index]
        weight_out = full_out[layer_index]

        def edge_block(summed, pieces):
            latent, sender_ids, receiver_ids, live_mask = pieces
            sender_table = (sender_ids[:, None] == extended_columns[None, :]).astype(jnp.bfloat16)
            receiver_table = (receiver_ids[:, None] == extended_columns[None, :]).astype(
                jnp.bfloat16
            )
            sender_rows = product(sender_table, extended).astype(jnp.bfloat16)
            receiver_rows = product(receiver_table, extended).astype(jnp.bfloat16)
            linear = product(latent, weight_in[:feature_width])
            linear = linear + product(sender_rows, weight_in[feature_width : 2 * feature_width])
            linear = linear + product(receiver_rows, weight_in[2 * feature_width :])
            edge_hidden = jnp.maximum(linear, 0.0).astype(jnp.bfloat16)
            message = jnp.where(
                live_mask[:, None], layer_norm(product(edge_hidden, weight_out)), 0.0
            ).astype(jnp.bfloat16)
            message = lax.optimization_barrier(message)
            renewed = (latent.astype(jnp.float32) + message.astype(jnp.float32)).astype(
                jnp.bfloat16
            )
            summed = summed + column_sum(receiver_table, message, False)
            return (summed, renewed)

        start_sums = jnp.zeros((extended_total, feature_width), jnp.float32)
        edge_pieces = (
            edges_now.reshape(block_count, block_rows, feature_width),
            sender_blocks,
            receiver_blocks,
            live_blocks,
        )
        summed, renewed_blocks = lax.scan(edge_block, start_sums, edge_pieces)
        edges_now = renewed_blocks.reshape(edge_rows, feature_width)
        returned = summed[node_total:].reshape(len(neighbour_offsets), -1, feature_width)
        owned_sums = return_sums(returned, pick_float, summed[:node_total])
        share_sum = lax.psum_scatter(owned_sums, "tp", scatter_dimension=0, tiled=True)
        aggregate = share_sum.astype(jnp.bfloat16)
        own_rows = lax.dynamic_slice_in_dim(nodes_now, first_row, share_rows, 0)
        linear_nodes = product(own_rows, node_first[layer_index][:feature_width]) + product(
            aggregate, node_first[layer_index][feature_width:]
        )
        node_hidden = jnp.maximum(linear_nodes, 0.0).astype(jnp.bfloat16)
        update = product(node_hidden, node_second[layer_index])
        renewed = (own_rows.astype(jnp.float32) + layer_norm(update)).astype(jnp.bfloat16)
        nodes_now = lax.all_gather(renewed, "tp", axis=0, tiled=True)
    return (nodes_now, edges_now)


def solution(mesh):
    return jax.shard_map(
        local,
        mesh=mesh,
        in_specs=(
            P("dom", None),
            P(("dom", "tp"), None),
            P(("dom", "tp")),
            P(("dom", "tp")),
            P(("dom", "tp")),
            P("dom", None, None),
            P(None, None, "tp"),
            P(None, "tp", None),
            P(None, None, "tp"),
            P(None, "tp", None),
        ),
        out_specs=(P("dom", None), P(("dom", "tp"), None)),
        check_vma=False,
    )
```

profile of v0, /device:TPU:0, one launch (start us, length us, event | category | flops | bytes accessed | tf_op | source)
XLA Modules:
  0.0 327.2 jit_solution(16853936986817779217)
XLA Ops:
  11.8 4.1 %collective-permute-start.1 = (bf16[128,128]{1,0:T(8,128)(2,1)S(1)}, bf16[128,128]{1,0:T(8,128)(2,1)S(1)}, u32[]{:S(2)}, u32[]{:S(2)}) collective-permute-start(bf16[128,128]{1,0:T(8,128)(2,1)S(1)} %get-tuple-element.557), channel_id=1, source_target_pairs={{0,30},{2,0},{4,2},{6,4},{8,6},{10,8},{12,10},{14,12},{16,14},{18,... | collective-permute-start | bytes 98312 | tf_op jit(solution)/shard_map/ppermute | solution.py:15
  15.9 4.7 %collective-permute-start.3 = (bf16[128,128]{1,0:T(8,128)(2,1)S(1)}, bf16[128,128]{1,0:T(8,128)(2,1)S(1)}, u32[]{:S(2)}, u32[]{:S(2)}) collective-permute-start(bf16[128,128]{1,0:T(8,128)(2,1)S(1)} %get-tuple-element.555), channel_id=1, source_target_pairs={{0,28},{2,30},{4,0},{6,2},{8,4},{10,6},{12,8},{14,10},{16,12},{18,... | collective-permute-start | bytes 98312 | tf_op jit(solution)/shard_map/ppermute | solution.py:15
  28.7 64.4 %while.42 = (s32[]{:T(128)}, f32[1536,128]{1,0:T(8,128)S(1)}, bf16[8,512,128]{2,1,0:T(8,128)(2,1)S(1)}, s32[8,512]{1,0:T(8,128)S(1)}, pred[8,512]{1,0:T(8,128)(4...) while((s32[]{:T(128)}, f32[1536,128]{1,0:T(8,128)S(1)}, ...), condition=%wide.region_3.4_spmd.clone.clone, body=%wide.region_0.3_spmd.clone.clone.sunk | while | flops 675021312 | bytes 5933195 | solution.py:140
  97.3 3.6 %collective-permute-done.5 = bf16[128,128]{1,0:T(8,128)(2,1)S(1)} collective-permute-done((bf16[128,128]{1,0:T(8,128)(2,1)S(1)}, bf16[128,128]{1,0:T(8,128)(2,1)S(1)}, u32[]{:S(2)}, u32[]{:S(2)}) %collective-permute-start.5) | collective-permute-done | bytes 32800 | tf_op jit(solution)/shard_map/ppermute | solution.py:15
  107.9 3.7 %reduce-scatter.4.cloned.1.call-done = f32[512,128]{1,0:T(8,128)} async-done(((f32[1024,128]{1,0:T(8,128)}), f32[512,128]{1,0:T(8,128)}) %reduce-scatter.4.cloned.1.call-update) | async-done | bytes 262160 | tf_op jit(solution)/shard_map/reduce_scatter | solution.py:144
  117.5 4.0 %collective-permute-start.9 = (bf16[128,128]{0,1:T(8,128)(2,1)S(1)}, bf16[128,128]{0,1:T(8,128)(2,1)S(1)}, u32[]{:S(2)}, u32[]{:S(2)}) collective-permute-start(bf16[128,128]{0,1:T(8,128)(2,1)S(1)} %get-tuple-element.553), channel_id=1, source_target_pairs={{0,30},{2,0},{4,2},{6,4},{8,6},{10,8},{12,10},{14,12},{16,14},{18,... | collective-permute-start | bytes 98312 | tf_op jit(solution)/shard_map/ppermute | solution.py:15
  121.5 4.7 %collective-permute-start.11 = (bf16[128,128]{0,1:T(8,128)(2,1)S(1)}, bf16[128,128]{0,1:T(8,128)(2,1)S(1)}, u32[]{:S(2)}, u32[]{:S(2)}) collective-permute-start(bf16[128,128]{0,1:T(8,128)(2,1)S(1)} %get-tuple-element.551), channel_id=1, source_target_pairs={{0,28},{2,30},{4,0},{6,2},{8,4},{10,6},{12,8},{14,10},{16,12},{18,... | collective-permute-start | bytes 98312 | tf_op jit(solution)/shard_map/ppermute | solution.py:15
  129.2 62.7 %while.43 = (s32[]{:T(128)}, f32[1536,128]{1,0:T(8,128)}, bf16[8,512,128]{2,1,0:T(8,128)(2,1)S(1)}, s32[8,512]{1,0:T(8,128)S(1)}, pred[8,512]{1,0:T(8,128)(4,1)S...) while((s32[]{:T(128)}, f32[1536,128]{1,0:T(8,128)}, ...), condition=%wide.region_10.11_spmd.clone.clone, body=%wide.region_7.10_spmd.clone.clone.sunk | while | flops 675021312 | bytes 5932687 | solution.py:140
  195.5 4.5 %collective-permute-start.14 = (bf16[128,128]{1,0:T(8,128)(2,1)S(1)}, bf16[128,128]{1,0:T(8,128)(2,1)S(1)}, u32[]{:S(2)}, u32[]{:S(2)}) collective-permute-start(bf16[128,128]{1,0:T(8,128)(2,1)S(1)} %get-tuple-element.538), channel_id=1, source_target_pairs={{0,28},{2,30},{4,0},{6,2},{8,4},{10,6},{12,8},{14,10},{16,12},{18,... | collective-permute-start | bytes 98312 | tf_op jit(solution)/shard_map/ppermute | solution.py:15
  200.0 3.2 collective-permute-done.13
  203.2 3.4 %collective-permute-done.15 = bf16[128,128]{1,0:T(8,128)(2,1)S(1)} collective-permute-done((bf16[128,128]{1,0:T(8,128)(2,1)S(1)}, bf16[128,128]{1,0:T(8,128)(2,1)S(1)}, u32[]{:S(2)}, u32[]{:S(2)}) %collective-permute-start.15) | collective-permute-done | bytes 32800 | tf_op jit(solution)/shard_map/ppermute | solution.py:15
  208.7 5.1 %reduce-scatter.6.cloned.1.call-done = f32[512,128]{1,0:T(8,128)} async-done(((f32[1024,128]{1,0:T(8,128)}), f32[512,128]{1,0:T(8,128)}) %reduce-scatter.6.cloned.1.call-update) | async-done | bytes 262160 | tf_op jit(solution)/shard_map/reduce_scatter | solution.py:144
  219.7 4.0 %collective-permute-start.17 = (bf16[128,128]{0,1:T(8,128)(2,1)S(1)}, bf16[128,128]{0,1:T(8,128)(2,1)S(1)}, u32[]{:S(2)}, u32[]{:S(2)}) collective-permute-start(bf16[128,128]{0,1:T(8,128)(2,1)S(1)} %get-tuple-element.549), channel_id=1, source_target_pairs={{0,30},{2,0},{4,2},{6,4},{8,6},{10,8},{12,10},{14,12},{16,14},{18,... | collective-permute-start | bytes 98312 | tf_op jit(solution)/shard_map/ppermute | solution.py:15
  223.7 4.7 %collective-permute-start.19 = (bf16[128,128]{0,1:T(8,128)(2,1)S(1)}, bf16[128,128]{0,1:T(8,128)(2,1)S(1)}, u32[]{:S(2)}, u32[]{:S(2)}) collective-permute-start(bf16[128,128]{0,1:T(8,128)(2,1)S(1)} %get-tuple-element.547), channel_id=1, source_target_pairs={{0,28},{2,30},{4,0},{6,2},{8,4},{10,6},{12,8},{14,10},{16,12},{18,... | collective-permute-start | bytes 98312 | tf_op jit(solution)/shard_map/ppermute | solution.py:15
  231.4 62.8 %while.44 = (s32[]{:T(128)}, f32[1536,128]{1,0:T(8,128)}, bf16[8,512,128]{2,1,0:T(8,128)(2,1)S(1)}, s32[8,512]{1,0:T(8,128)S(1)}, pred[8,512]{1,0:T(8,128)(4,1)S...) while((s32[]{:T(128)}, f32[1536,128]{1,0:T(8,128)}, ...), condition=%wide.region_17.18_spmd.clone.clone, body=%wide.region_14.17_spmd.clone.clone.sunk | while | flops 675021312 | bytes 5932687 | solution.py:140
  243.1 3.1 fusion.256
  251.1 3.1 fusion.256
  259.1 3.1 fusion.256
  267.1 3.1 fusion.256
  275.1 3.1 fusion.256
  298.0 4.5 %collective-permute-start.22 = (bf16[128,128]{1,0:T(8,128)(2,1)S(1)}, bf16[128,128]{1,0:T(8,128)(2,1)S(1)}, u32[]{:S(2)}, u32[]{:S(2)}) collective-permute-start(bf16[128,128]{1,0:T(8,128)(2,1)S(1)} %get-tuple-element.534), channel_id=1, source_target_pairs={{0,28},{2,30},{4,0},{6,2},{8,4},{10,6},{12,8},{14,10},{16,12},{18,... | collective-permute-start | bytes 98312 | tf_op jit(solution)/shard_map/ppermute | solution.py:15
  302.5 3.2 collective-permute-done.21
  305.7 3.4 %collective-permute-done.23 = bf16[128,128]{1,0:T(8,128)(2,1)S(1)} collective-permute-done((bf16[128,128]{1,0:T(8,128)(2,1)S(1)}, bf16[128,128]{1,0:T(8,128)(2,1)S(1)}, u32[]{:S(2)}, u32[]{:S(2)}) %collective-permute-start.23) | collective-permute-done | bytes 32800 | tf_op jit(solution)/shard_map/ppermute | solution.py:15
  311.8 4.6 %reduce-scatter.8.cloned.1.call-done = f32[512,128]{1,0:T(8,128)} async-done(((f32[1024,128]{1,0:T(8,128)}), f32[512,128]{1,0:T(8,128)}) %reduce-scatter.8.cloned.1.call-update) | async-done | bytes 262160 | tf_op jit(solution)/shard_map/reduce_scatter | solution.py:144
  (448 shorter events, 229.8 us)
Async XLA Ops:
  7.2 104.5 %reduce-scatter.4.cloned.1.call-start = ((), (), s32[]{:S(2)}) async-start(), calls=%async_computation.3 | async-start | bytes 786432 | tf_op jit(solution)/shard_map/reduce_scatter | solution.py:144
  8.8 17.3 %collective-permute-start = (bf16[128,128]{1,0:T(8,128)(2,1)S(1)}, bf16[128,128]{1,0:T(8,128)(2,1)S(1)}, u32[]{:S(2)}, u32[]{:S(2)}) collective-permute-start(bf16[128,128]{1,0:T(8,128)(2,1)S(1)} %get-tuple-element.558), channel_id=1, source_target_pairs={{0,2},{2,4},{4,6},{6,8},{8,10},{10,12},{12,14},{14,16},{16,18},{18... | collective-permute-start | bytes 98312 | tf_op jit(solution)/shard_map/ppermute | solution.py:15
  11.8 14.9 %collective-permute-start.1 = (bf16[128,128]{1,0:T(8,128)(2,1)S(1)}, bf16[128,128]{1,0:T(8,128)(2,1)S(1)}, u32[]{:S(2)}, u32[]{:S(2)}) collective-permute-start(bf16[128,128]{1,0:T(8,128)(2,1)S(1)} %get-tuple-element.557), channel_id=1, source_target_pairs={{0,30},{2,0},{4,2},{6,4},{8,6},{10,8},{12,10},{14,12},{16,14},{18,... | collective-permute-start | bytes 98312 | tf_op jit(solution)/shard_map/ppermute | solution.py:15
  15.9 11.5 %collective-permute-start.2 = (bf16[128,128]{1,0:T(8,128)(2,1)S(1)}, bf16[128,128]{1,0:T(8,128)(2,1)S(1)}, u32[]{:S(2)}, u32[]{:S(2)}) collective-permute-start(bf16[128,128]{1,0:T(8,128)(2,1)S(1)} %get-tuple-element.556), channel_id=1, source_target_pairs={{0,4},{2,6},{4,8},{6,10},{8,12},{10,14},{12,16},{14,18},{16,20},{1... | collective-permute-start | bytes 98312 | tf_op jit(solution)/shard_map/ppermute | solution.py:15
  15.9 12.1 %collective-permute-start.3 = (bf16[128,128]{1,0:T(8,128)(2,1)S(1)}, bf16[128,128]{1,0:T(8,128)(2,1)S(1)}, u32[]{:S(2)}, u32[]{:S(2)}) collective-permute-start(bf16[128,128]{1,0:T(8,128)(2,1)S(1)} %get-tuple-element.555), channel_id=1, source_target_pairs={{0,28},{2,30},{4,0},{6,2},{8,4},{10,6},{12,8},{14,10},{16,12},{18,... | collective-permute-start | bytes 98312 | tf_op jit(solution)/shard_map/ppermute | solution.py:15
  93.3 7.6 %collective-permute-start.5 = (bf16[128,128]{1,0:T(8,128)(2,1)S(1)}, bf16[128,128]{1,0:T(8,128)(2,1)S(1)}, u32[]{:S(2)}, u32[]{:S(2)}) collective-permute-start(bf16[128,128]{1,0:T(8,128)(2,1)S(1)} %get-tuple-element.543), channel_id=1, source_target_pairs={{0,2},{2,4},{4,6},{6,8},{8,10},{10,12},{12,14},{14,16},{16,18},{18... | collective-permute-start | bytes 98312 | tf_op jit(solution)/shard_map/ppermute | solution.py:15
  95.3 6.6 %collective-permute-start.7 = (bf16[128,128]{1,0:T(8,128)(2,1)S(1)}, bf16[128,128]{1,0:T(8,128)(2,1)S(1)}, u32[]{:S(2)}, u32[]{:S(2)}) collective-permute-start(bf16[128,128]{1,0:T(8,128)(2,1)S(1)} %get-tuple-element.541), channel_id=1, source_target_pairs={{0,4},{2,6},{4,8},{6,10},{8,12},{10,14},{12,16},{14,18},{16,20},{1... | collective-permute-start | bytes 98312 | tf_op jit(solution)/shard_map/ppermute | solution.py:15
  103.6 110.2 %reduce-scatter.6.cloned.1.call-start = ((), (), s32[]{:S(2)}) async-start(), calls=%async_computation.4 | async-start | bytes 786432 | tf_op jit(solution)/shard_map/reduce_scatter | solution.py:144
  115.8 10.5 %collective-permute-start.8 = (bf16[128,128]{0,1:T(8,128)(2,1)S(1)}, bf16[128,128]{0,1:T(8,128)(2,1)S(1)}, u32[]{:S(2)}, u32[]{:S(2)}) collective-permute-start(bf16[128,128]{0,1:T(8,128)(2,1)S(1)} %get-tuple-element.554), channel_id=1, source_target_pairs={{0,2},{2,4},{4,6},{6,8},{8,10},{10,12},{12,14},{14,16},{16,18},{18... | collective-permute-start | bytes 98312 | tf_op jit(solution)/shard_map/ppermute | solution.py:15
  117.5 8.7 %collective-permute-start.9 = (bf16[128,128]{0,1:T(8,128)(2,1)S(1)}, bf16[128,128]{0,1:T(8,128)(2,1)S(1)}, u32[]{:S(2)}, u32[]{:S(2)}) collective-permute-start(bf16[128,128]{0,1:T(8,128)(2,1)S(1)} %get-tuple-element.553), channel_id=1, source_target_pairs={{0,30},{2,0},{4,2},{6,4},{8,6},{10,8},{12,10},{14,12},{16,14},{18,... | collective-permute-start | bytes 98312 | tf_op jit(solution)/shard_map/ppermute | solution.py:15
  121.5 6.6 %collective-permute-start.10 = (bf16[128,128]{0,1:T(8,128)(2,1)S(1)}, bf16[128,128]{0,1:T(8,128)(2,1)S(1)}, u32[]{:S(2)}, u32[]{:S(2)}) collective-permute-start(bf16[128,128]{0,1:T(8,128)(2,1)S(1)} %get-tuple-element.552), channel_id=1, source_target_pairs={{0,4},{2,6},{4,8},{6,10},{8,12},{10,14},{12,16},{14,18},{16,20},{1... | collective-permute-start | bytes 98312 | tf_op jit(solution)/shard_map/ppermute | solution.py:15
  121.5 6.6 %collective-permute-start.11 = (bf16[128,128]{0,1:T(8,128)(2,1)S(1)}, bf16[128,128]{0,1:T(8,128)(2,1)S(1)}, u32[]{:S(2)}, u32[]{:S(2)}) collective-permute-start(bf16[128,128]{0,1:T(8,128)(2,1)S(1)} %get-tuple-element.551), channel_id=1, source_target_pairs={{0,28},{2,30},{4,0},{6,2},{8,4},{10,6},{12,8},{14,10},{16,12},{18,... | collective-permute-start | bytes 98312 | tf_op jit(solution)/shard_map/ppermute | solution.py:15
  193.2 6.8 %collective-permute-start.12 = (bf16[128,128]{1,0:T(8,128)(2,1)S(1)}, bf16[128,128]{1,0:T(8,128)(2,1)S(1)}, u32[]{:S(2)}, u32[]{:S(2)}) collective-permute-start(bf16[128,128]{1,0:T(8,128)(2,1)S(1)} %get-tuple-element.536), channel_id=1, source_target_pairs={{0,30},{2,0},{4,2},{6,4},{8,6},{10,8},{12,10},{14,12},{16,14},{18,... | collective-permute-start | bytes 98312 | tf_op jit(solution)/shard_map/ppermute | solution.py:15
  195.5 7.7 %collective-permute-start.13 = (bf16[128,128]{1,0:T(8,128)(2,1)S(1)}, bf16[128,128]{1,0:T(8,128)(2,1)S(1)}, u32[]{:S(2)}, u32[]{:S(2)}) collective-permute-start(bf16[128,128]{1,0:T(8,128)(2,1)S(1)} %get-tuple-element.539), channel_id=1, source_target_pairs={{0,2},{2,4},{4,6},{6,8},{8,10},{10,12},{12,14},{14,16},{16,18},{18... | collective-permute-start | bytes 98312 | tf_op jit(solution)/shard_map/ppermute | solution.py:15
  195.5 7.7 %collective-permute-start.14 = (bf16[128,128]{1,0:T(8,128)(2,1)S(1)}, bf16[128,128]{1,0:T(8,128)(2,1)S(1)}, u32[]{:S(2)}, u32[]{:S(2)}) collective-permute-start(bf16[128,128]{1,0:T(8,128)(2,1)S(1)} %get-tuple-element.538), channel_id=1, source_target_pairs={{0,28},{2,30},{4,0},{6,2},{8,4},{10,6},{12,8},{14,10},{16,12},{18,... | collective-permute-start | bytes 98312 | tf_op jit(solution)/shard_map/ppermute | solution.py:15
  200.0 6.6 %collective-permute-start.15 = (bf16[128,128]{1,0:T(8,128)(2,1)S(1)}, bf16[128,128]{1,0:T(8,128)(2,1)S(1)}, u32[]{:S(2)}, u32[]{:S(2)}) collective-permute-start(bf16[128,128]{1,0:T(8,128)(2,1)S(1)} %get-tuple-element.537), channel_id=1, source_target_pairs={{0,4},{2,6},{4,8},{6,10},{8,12},{10,14},{12,16},{14,18},{16,20},{1... | collective-permute-start | bytes 98312 | tf_op jit(solution)/shard_map/ppermute | solution.py:15
  208.3 108.1 %reduce-scatter.8.cloned.1.call-start = ((), (), s32[]{:S(2)}) async-start(), calls=%async_computation.5 | async-start | bytes 786432 | tf_op jit(solution)/shard_map/reduce_scatter | solution.py:144
  217.9 10.5 %collective-permute-start.16 = (bf16[128,128]{0,1:T(8,128)(2,1)S(1)}, bf16[128,128]{0,1:T(8,128)(2,1)S(1)}, u32[]{:S(2)}, u32[]{:S(2)}) collective-permute-start(bf16[128,128]{0,1:T(8,128)(2,1)S(1)} %get-tuple-element.550), channel_id=1, source_target_pairs={{0,2},{2,4},{4,6},{6,8},{8,10},{10,12},{12,14},{14,16},{16,18},{18... | collective-permute-start | bytes 98312 | tf_op jit(solution)/shard_map/ppermute | solution.py:15
  219.7 8.7 %collective-permute-start.17 = (bf16[128,128]{0,1:T(8,128)(2,1)S(1)}, bf16[128,128]{0,1:T(8,128)(2,1)S(1)}, u32[]{:S(2)}, u32[]{:S(2)}) collective-permute-start(bf16[128,128]{0,1:T(8,128)(2,1)S(1)} %get-tuple-element.549), channel_id=1, source_target_pairs={{0,30},{2,0},{4,2},{6,4},{8,6},{10,8},{12,10},{14,12},{16,14},{18,... | collective-permute-start | bytes 98312 | tf_op jit(solution)/shard_map/ppermute | solution.py:15
  223.7 6.6 %collective-permute-start.18 = (bf16[128,128]{0,1:T(8,128)(2,1)S(1)}, bf16[128,128]{0,1:T(8,128)(2,1)S(1)}, u32[]{:S(2)}, u32[]{:S(2)}) collective-permute-start(bf16[128,128]{0,1:T(8,128)(2,1)S(1)} %get-tuple-element.548), channel_id=1, source_target_pairs={{0,4},{2,6},{4,8},{6,10},{8,12},{10,14},{12,16},{14,18},{16,20},{1... | collective-permute-start | bytes 98312 | tf_op jit(solution)/shard_map/ppermute | solution.py:15
  223.7 6.6 %collective-permute-start.19 = (bf16[128,128]{0,1:T(8,128)(2,1)S(1)}, bf16[128,128]{0,1:T(8,128)(2,1)S(1)}, u32[]{:S(2)}, u32[]{:S(2)}) collective-permute-start(bf16[128,128]{0,1:T(8,128)(2,1)S(1)} %get-tuple-element.547), channel_id=1, source_target_pairs={{0,28},{2,30},{4,0},{6,2},{8,4},{10,6},{12,8},{14,10},{16,12},{18,... | collective-permute-start | bytes 98312 | tf_op jit(solution)/shard_map/ppermute | solution.py:15
  295.8 6.8 %collective-permute-start.20 = (bf16[128,128]{1,0:T(8,128)(2,1)S(1)}, bf16[128,128]{1,0:T(8,128)(2,1)S(1)}, u32[]{:S(2)}, u32[]{:S(2)}) collective-permute-start(bf16[128,128]{1,0:T(8,128)(2,1)S(1)} %get-tuple-element.532), channel_id=1, source_target_pairs={{0,30},{2,0},{4,2},{6,4},{8,6},{10,8},{12,10},{14,12},{16,14},{18,... | collective-permute-start | bytes 98312 | tf_op jit(solution)/shard_map/ppermute | solution.py:15
  298.0 7.7 %collective-permute-start.21 = (bf16[128,128]{1,0:T(8,128)(2,1)S(1)}, bf16[128,128]{1,0:T(8,128)(2,1)S(1)}, u32[]{:S(2)}, u32[]{:S(2)}) collective-permute-start(bf16[128,128]{1,0:T(8,128)(2,1)S(1)} %get-tuple-element.535), channel_id=1, source_target_pairs={{0,2},{2,4},{4,6},{6,8},{8,10},{10,12},{12,14},{14,16},{16,18},{18... | collective-permute-start | bytes 98312 | tf_op jit(solution)/shard_map/ppermute | solution.py:15
  298.0 7.7 %collective-permute-start.22 = (bf16[128,128]{1,0:T(8,128)(2,1)S(1)}, bf16[128,128]{1,0:T(8,128)(2,1)S(1)}, u32[]{:S(2)}, u32[]{:S(2)}) collective-permute-start(bf16[128,128]{1,0:T(8,128)(2,1)S(1)} %get-tuple-element.534), channel_id=1, source_target_pairs={{0,28},{2,30},{4,0},{6,2},{8,4},{10,6},{12,8},{14,10},{16,12},{18,... | collective-permute-start | bytes 98312 | tf_op jit(solution)/shard_map/ppermute | solution.py:15
  (16 other events, 358.8 us)
Sparse Core Ops, SparseCore 0:
  103.7 7.9 reduce-scatter.3
  208.4 5.3 reduce-scatter.5
  310.9 5.4 reduce-scatter.7
where the time goes:
time: 331 us; the launch traced here: 327 us
  matrix products  176 us (53%)
  starting transfers between devices  50.5 us (15%)
  waiting for transfers between devices  35 us (11%)
  other arithmetic  24.3 us (7%)
  between operations  14.8 us (4%)
  blocking collectives  13.7 us (4%)
  local copies, waits for them, and re-layouts  11 us (3%)
    dot_general x105, matrix products, product(): jnp.dot(first_operand, second_operand, preferred_element_type=jnp.float32)  113 us
    dot_general x24, matrix products, column_sum(): lax.dot_general(table, values, (((0,), (0,)), ((), ())), preferred_elemen...  58.3 us
    ppermute x24, starting transfers between devices, from_behind(): lax.ppermute(array, axis, [(i, (i + by) % length) for i in range(length)])  50.3 us
    ppermute x24, waiting for transfers between devices, from_behind(): lax.ppermute(array, axis, [(i, (i + by) % length) for i in range(length)])  21.5 us
    reduce_scatter x3, waiting for transfers between devices, local(): lax.psum_scatter(owned_sums, 'tp', scatter_dimension=0, tiled=True)  13.5 us
    dynamic_update_slice x24, other arithmetic, local(): summed, renewed_blocks = lax.scan(edge_block, start_sums, edge_pieces)  8.68 us
  transfers between devices with their start and end apart: 27, of which 11 were waited for; matrix products, arithmetic and copies ran while one was open for 1% of the time, Pallas kernels for 0%

commit v1 on v0

--- a/solution.py
+++ b/solution.py
@@ -1,6 +1,10 @@
+import functools
+
 import jax
 import jax.numpy as jnp
 from jax import lax
+from jax.experimental import pallas as pl
+from jax.experimental.pallas import tpu as pltpu
 from jax.sharding import PartitionSpec as P
 
 LAYERS = 3
@@ -60,6 +64,92 @@
         for neighbour, offset in enumerate(neighbour_offsets)
     ]
     return owned_sums + column_sum(pick_float, jnp.concatenate(arrived, axis=0), True)
+
+
+LOW = 256
+BLOCK = 1024
+
+
+def edge_kernel(
+    count_ref, ext_ref, latent_ref, ids_ref, win_ref, wout_ref, renewed_ref, summed_ref,
+    send_table, recv_table, sums,
+):
+    width = ext_ref.shape[1]
+    high = ext_ref.shape[0] // LOW
+    rows = latent_ref.shape[0]
+    block = min(BLOCK, rows)
+    for h in range(high):
+        part = ext_ref[h * LOW : (h + 1) * LOW, :]
+        lanes = slice(h * width, (h + 1) * width)
+        send_table[:, lanes] = product(part, win_ref[width : 2 * width, :]).astype(jnp.bfloat16)
+        recv_table[:, lanes] = product(part, win_ref[2 * width :, :]).astype(jnp.bfloat16)
+    sums[...] = jnp.zeros_like(sums)
+    weight_out = wout_ref[...]
+    count = count_ref[0]
+
+    def gathered(ids, table):
+        low = ids & (LOW - 1)
+        lane = lax.broadcasted_iota(jnp.int32, (block, width), 1)
+        halves = [(low == lane + c).astype(jnp.bfloat16) for c in range(0, LOW, width)]
+        all_rows = product(jnp.concatenate(halves, axis=1), table[...])
+        top = ids // LOW
+        found = all_rows[:, :width]
+        for h in range(1, high):
+            found = jnp.where(top == h, all_rows[:, h * width : (h + 1) * width], found)
+        return found
+
+    def step(i, carry):
+        at = pl.ds(pl.multiple_of(i * block, block), block)
+        send_row = ids_ref[0:1, at]
+        recv_row = ids_ref[1:2, at]
+        send_ids = jnp.broadcast_to(send_row, (width, block)).T
+        recv_ids = jnp.broadcast_to(recv_row, (width, block)).T
+        latent = latent_ref[at, :]
+        linear = product(latent, win_ref[:width, :])
+        linear = linear + gathered(send_ids, send_table) + gathered(recv_ids, recv_table)
+        hidden = jnp.maximum(linear, 0.0).astype(jnp.bfloat16)
+        message = layer_norm(product(hidden, weight_out))
+        position = lax.broadcasted_iota(jnp.int32, (block, width), 0) + i * block
+        message = jnp.where(position < count, message, 0.0).astype(jnp.bfloat16)
+        wide = message.astype(jnp.float32)
+        renewed_ref[at, :] = (latent.astype(jnp.float32) + wide).astype(jnp.bfloat16)
+        top = recv_ids // LOW
+        spread = jnp.concatenate(
+            [jnp.where(top == h, wide, 0.0).astype(jnp.bfloat16) for h in range(high)], axis=1
+        )
+        low_row = jnp.broadcast_to(recv_row & (LOW - 1), (LOW, block))
+        table = (low_row == lax.broadcasted_iota(jnp.int32, (LOW, block), 0)).astype(jnp.bfloat16)
+        sums[...] += product(table, spread)
+        return carry
+
+    lax.fori_loop(0, rows // block, step, 0)
+    for h in range(high):
+        summed_ref[h * LOW : (h + 1) * LOW, :] = sums[:, h * width : (h + 1) * width]
+
+
+def edge_stage(extended, edges_now, id_rows, edge_count, weight_in, weight_out):
+    total, width = extended.shape
+    rows = edges_now.shape[0]
+    high = total // LOW
+    whole = pl.BlockSpec(memory_space=pltpu.VMEM)
+    return pl.pallas_call(
+        edge_kernel,
+        out_shape=(
+            jax.ShapeDtypeStruct((rows, width), jnp.bfloat16),
+            jax.ShapeDtypeStruct((total, width), jnp.float32),
+        ),
+        in_specs=[pl.BlockSpec(memory_space=pltpu.SMEM)] + [whole] * 5,
+        out_specs=(whole, whole),
+        scratch_shapes=[
+            pltpu.VMEM((LOW, high * width), jnp.bfloat16),
+            pltpu.VMEM((LOW, high * width), jnp.bfloat16),
+            pltpu.VMEM((LOW, high * width), jnp.float32),
+        ],
+        compiler_params=pltpu.CompilerParams(vmem_limit_bytes=48 * 1024 * 1024),
+        cost_estimate=pl.CostEstimate(
+            flops=8 * rows * total * width, bytes_accessed=4 * rows * width, transcendentals=rows
+        ),
+    )(edge_count, extended, edges_now, id_rows, weight_in, weight_out)
 
 
 def local(
@@ -78,20 +168,13 @@
     node_total = node_latent.shape[0]
     share_rows = node_total // lax.axis_size("tp")
     first_row = lax.axis_index("tp") * share_rows
-    edge_rows = edge_latent.shape[0]
-    block_rows = min(512, edge_rows)
-    block_count = edge_rows // block_rows
     flat_index = send_index[0].reshape(-1)
     halo_total = flat_index.shape[0]
     extended_total = node_total + halo_total
     pick_match = flat_index[:, None] == jnp.arange(node_total, dtype=jnp.int32)[None, :]
     pick_table = pick_match.astype(jnp.bfloat16)
     pick_float = pick_match.astype(jnp.float32)
-    live_edges = jnp.arange(edge_rows, dtype=jnp.int32) < edge_count[0]
-    sender_blocks = edge_sender.reshape(block_count, block_rows)
-    receiver_blocks = edge_receiver.reshape(block_count, block_rows)
-    live_blocks = live_edges.reshape(block_count, block_rows)
-    extended_columns = jnp.arange(extended_total, dtype=jnp.int32)
+    id_rows = jnp.stack([edge_sender, edge_receiver])
     full_in, full_out = (
         lax.all_gather(edge_in, "tp", axis=2, tiled=True),
         lax.all_gather(edge_out, "tp", axis=1, tiled=True),
@@ -105,40 +188,9 @@
     for layer_index in range(LAYERS):
         halo_rows = fetch_halo(nodes_now, pick_table)
         extended = jnp.concatenate([nodes_now, halo_rows], axis=0)
-        weight_in = full_in[layer_index]
-        weight_out = full_out[layer_index]
-
-        def edge_block(summed, pieces):
-            latent, sender_ids, receiver_ids, live_mask = pieces
-            sender_table = (sender_ids[:, None] == extended_columns[None, :]).astype(jnp.bfloat16)
-            receiver_table = (receiver_ids[:, None] == extended_columns[None, :]).astype(
-                jnp.bfloat16
-            )
-            sender_rows = product(sender_table, extended).astype(jnp.bfloat16)
-            receiver_rows = product(receiver_table, extended).astype(jnp.bfloat16)
-            linear = product(latent, weight_in[:feature_width])
-            linear = linear + product(sender_rows, weight_in[feature_width : 2 * feature_width])
-            linear = linear + product(receiver_rows, weight_in[2 * feature_width :])
-            edge_hidden = jnp.maximum(linear, 0.0).astype(jnp.bfloat16)
-            message = jnp.where(
-                live_mask[:, None], layer_norm(product(edge_hidden, weight_out)), 0.0
-            ).astype(jnp.bfloat16)
-            message = lax.optimization_barrier(message)
-            renewed = (latent.astype(jnp.float32) + message.astype(jnp.float32)).astype(
-                jnp.bfloat16
-            )
-            summed = summed + column_sum(receiver_table, message, False)
-            return (summed, renewed)
-
-        start_sums = jnp.zeros((extended_total, feature_width), jnp.float32)
-        edge_pieces = (
-            edges_now.reshape(block_count, block_rows, feature_width),
-            sender_blocks,
-            receiver_blocks,
-            live_blocks,
-        )
-        summed, renewed_blocks = lax.scan(edge_block, start_sums, edge_pieces)
-        edges_now = renewed_blocks.reshape(edge_rows, feature_width)
+        edges_now, summed = edge_stage(
+            extended, edges_now, id_rows, edge_count, full_in[layer_index], full_out[layer_index]
+        )
         returned = summed[node_total:].reshape(len(neighbour_offsets), -1, feature_width)
         owned_sums = return_sums(returned, pick_float, summed[:node_total])
         share_sum = lax.psum_scatter(owned_sums, "tp", scatter_dimension=0, tiled=True)

time: 331 us -> 165 us (0.50); the launches traced: 327 us -> 165 us
  matrix products: 176 us -> 11.9 us
  Pallas kernels: 0 us -> 34.2 us
  other arithmetic: 24.3 us -> 1.52 us
  local copies, waits for them, and re-layouts: 11 us -> 1.76 us
    dot_general x105 -> x9, matrix products: 113 us -> 7.1 us  [product(): jnp.dot(first_operand, second_operand, preferred_element_type=jnp.float32)]
    dot_general x24 -> x0, matrix products: 58.3 us -> none  [column_sum(): lax.dot_general(table, values, (((0,), (0,)), ((), ())), preferred_elemen...]
    pallas_call x0 -> x3, Pallas kernels: none -> 34.2 us  [edge_stage(): pl.pallas_call(edge_kernel, out_shape=(jax.ShapeDtypeStruct((rows, width)...]
    dynamic_update_slice x24 -> x0, other arithmetic: 8.68 us -> none  [local(): summed, renewed_blocks = lax.scan(edge_block, start_sums, edge_pieces)]
    convert_element_type x24 -> x0, other arithmetic: 6.56 us -> none  [edge_block(): message = jnp.where(live_mask[:, None], layer_norm(product(edge_hidden, w...]
    reduce_sum x27 -> x3, other arithmetic: 5.73 us -> 0.7 us  [layer_norm(): spread = jnp.mean(centred * centred, axis=-1, keepdims=True)]
    unnamed x46 -> x34, local copies, waits for them, and re-layouts: 5.91 us -> 1.26 us
where the time goes in v1:
time: 165 us
  starting transfers between devices  50.7 us (31%)
  waiting for transfers between devices  35.8 us (22%)
  Pallas kernels  34.2 us (21%)
  between operations  14.9 us (9%)
  blocking collectives  13.8 us (8%)
  matrix products  11.9 us (7%)
  local copies, waits for them, and re-layouts  1.76 us (1%)
    ppermute x24, starting transfers between devices, from_behind(): lax.ppermute(array, axis, [(i, (i + by) % length) for i in range(length)])  50.4 us
    pallas_call x3, Pallas kernels, edge_stage(): pl.pallas_call(edge_kernel, out_shape=(jax.ShapeDtypeStruct((rows, width)...  34.2 us
    ppermute x24, waiting for transfers between devices, from_behind(): lax.ppermute(array, axis, [(i, (i + by) % length) for i in range(length)])  23.1 us
    reduce_scatter x3, waiting for transfers between devices, local(): lax.psum_scatter(owned_sums, 'tp', scatter_dimension=0, tiled=True)  12.7 us
    dot_general x9, matrix products, product(): jnp.dot(first_operand, second_operand, preferred_element_type=jnp.float32)  7.1 us
    all_gather x3, blocking collectives, local(): nodes_now = lax.all_gather(renewed, 'tp', axis=0, tiled=True)  5.98 us
    dot_general x3, matrix products, column_sum(): lax.dot_general(table, values, (((0,), (0,)), ((), ())), precision=lax.Pr...  4.85 us
  transfers between devices with their start and end apart: 27, of which 11 were waited for; matrix products, arithmetic and copies ran while one was open for 1% of the time, Pallas kernels for 0%

profile of v1, /device:TPU:0, one launch (start us, length us, event | category | flops | bytes accessed | tf_op | source)
XLA Modules:
  0.0 164.6 jit_solution(13941533592509646482)
XLA Ops:
  8.8 3.0 %collective-permute-start = (bf16[128,128]{1,0:T(8,128)(2,1)S(1)}, bf16[128,128]{1,0:T(8,128)(2,1)S(1)}, u32[]{:S(2)}, u32[]{:S(2)}) collective-permute-start(bf16[128,128]{1,0:T(8,128)(2,1)S(1)} %get-tuple-element.40), channel_id=1, source_target_pairs={{0,2},{2,4},{4,6},{6,8},{8,10},{10,12},{12,14},{14,16},{16,18},{18... | collective-permute-start | bytes 98312 | tf_op jit(solution)/shard_map/ppermute | solution.py:19
  11.8 4.1 %collective-permute-start.1 = (bf16[128,128]{1,0:T(8,128)(2,1)S(1)}, bf16[128,128]{1,0:T(8,128)(2,1)S(1)}, u32[]{:S(2)}, u32[]{:S(2)}) collective-permute-start(bf16[128,128]{1,0:T(8,128)(2,1)S(1)} %get-tuple-element.39), channel_id=1, source_target_pairs={{0,30},{2,0},{4,2},{6,4},{8,6},{10,8},{12,10},{14,12},{16,14},{18,... | collective-permute-start | bytes 98312 | tf_op jit(solution)/shard_map/ppermute | solution.py:19
  15.9 4.7 %collective-permute-start.3 = (bf16[128,128]{1,0:T(8,128)(2,1)S(1)}, bf16[128,128]{1,0:T(8,128)(2,1)S(1)}, u32[]{:S(2)}, u32[]{:S(2)}) collective-permute-start(bf16[128,128]{1,0:T(8,128)(2,1)S(1)} %get-tuple-element.37), channel_id=1, source_target_pairs={{0,28},{2,30},{4,0},{6,2},{8,4},{10,6},{12,8},{14,10},{16,12},{18,... | collective-permute-start | bytes 98312 | tf_op jit(solution)/shard_map/ppermute | solution.py:19
  25.7 11.2 %shard_map.113 = (bf16[4096,128]{1,0:T(8,128)(2,1)S(1)}, f32[1536,128]{1,0:T(8,128)S(1)}) custom-call(s32[1]{0:T(128)S(6)} %copy.38.count_ref, bf16[1536,128]{1,0:T(8,128)(2,1)S(1)} %constant_dynamic-update-slice_fusion.ext_ref, bf16[4096,128]{1,0:T(8,128)(2,1)S(1)} %copy-done, s32[2,4096]{1,0:T(2,128)S(1)} %pad_add_fusion.ids_ref, ...), custom_call_target="tpu_custom_call" | custom-call | flops 6442450944 | bytes 2097152 | tf_op jit(solution)/shard_map/pallas_call | solution.py:135
  37.1 2.0 %collective-permute-start.5 = (bf16[128,128]{1,0:T(8,128)(2,1)S(1)}, bf16[128,128]{1,0:T(8,128)(2,1)S(1)}, u32[]{:S(2)}, u32[]{:S(2)}) collective-permute-start(bf16[128,128]{1,0:T(8,128)(2,1)S(1)} %get-tuple-element.25), channel_id=1, source_target_pairs={{0,2},{2,4},{4,6},{6,8},{8,10},{10,12},{12,14},{14,16},{16,18},{18... | collective-permute-start | bytes 98312 | tf_op jit(solution)/shard_map/ppermute | solution.py:19
  41.1 3.6 %collective-permute-done.5 = bf16[128,128]{1,0:T(8,128)(2,1)S(1)} collective-permute-done((bf16[128,128]{1,0:T(8,128)(2,1)S(1)}, bf16[128,128]{1,0:T(8,128)(2,1)S(1)}, u32[]{:S(2)}, u32[]{:S(2)}) %collective-permute-start.5) | collective-permute-done | bytes 32800 | tf_op jit(solution)/shard_map/ppermute | solution.py:19
  44.7 2.6 %collective-permute-done.7 = bf16[128,128]{1,0:T(8,128)(2,1)S(1)} collective-permute-done((bf16[128,128]{1,0:T(8,128)(2,1)S(1)}, bf16[128,128]{1,0:T(8,128)(2,1)S(1)}, u32[]{:S(2)}, u32[]{:S(2)}) %collective-permute-start.7) | collective-permute-done | bytes 32800 | tf_op jit(solution)/shard_map/ppermute | solution.py:19
  53.1 2.3 %reduce-scatter.4.cloned.1.call-done = f32[512,128]{1,0:T(8,128)} async-done(((f32[1024,128]{1,0:T(8,128)}), f32[512,128]{1,0:T(8,128)}) %reduce-scatter.4.cloned.1.call-update) | async-done | bytes 262160 | tf_op jit(solution)/shard_map/reduce_scatter | solution.py:196
  61.7 3.9 %collective-permute-start.9 = (bf16[128,128]{1,0:T(8,128)(2,1)S(1)}, bf16[128,128]{1,0:T(8,128)(2,1)S(1)}, u32[]{:S(2)}, u32[]{:S(2)}) collective-permute-start(bf16[128,128]{1,0:T(8,128)(2,1)S(1)} %get-tuple-element.35), channel_id=1, source_target_pairs={{0,30},{2,0},{4,2},{6,4},{8,6},{10,8},{12,10},{14,12},{16,14},{18,... | collective-permute-start | bytes 98312 | tf_op jit(solution)/shard_map/ppermute | solution.py:19
  65.6 4.7 %collective-permute-start.11 = (bf16[128,128]{1,0:T(8,128)(2,1)S(1)}, bf16[128,128]{1,0:T(8,128)(2,1)S(1)}, u32[]{:S(2)}, u32[]{:S(2)}) collective-permute-start(bf16[128,128]{1,0:T(8,128)(2,1)S(1)} %get-tuple-element.33), channel_id=1, source_target_pairs={{0,28},{2,30},{4,0},{6,2},{8,4},{10,6},{12,8},{14,10},{16,12},{18,... | collective-permute-start | bytes 98312 | tf_op jit(solution)/shard_map/ppermute | solution.py:19
  72.3 11.2 %shard_map.114 = (bf16[4096,128]{1,0:T(8,128)(2,1)S(1)}, f32[1536,128]{1,0:T(8,128)S(1)}) custom-call(s32[1]{0:T(128)S(6)} %copy.38.count_ref, bf16[1536,128]{1,0:T(8,128)(2,1)S(1)} %constant_dynamic-update-slice_fusion.5.ext_ref, bf16[4096,128]{1,0:T(8,128)(2,1)S(1)} %get-tuple-element.9.latent_ref, s32[2,4096]{1,0:T(2,128)S(1)} %pad_add_fusion.ids_ref, ...), custom_call_target="tpu_custom_call" | custom-call | flops 6442450944 | bytes 2097152 | tf_op jit(solution)/shard_map/pallas_call | solution.py:135
  83.6 2.3 %collective-permute-start.12 = (bf16[128,128]{1,0:T(8,128)(2,1)S(1)}, bf16[128,128]{1,0:T(8,128)(2,1)S(1)}, u32[]{:S(2)}, u32[]{:S(2)}) collective-permute-start(bf16[128,128]{1,0:T(8,128)(2,1)S(1)} %get-tuple-element.18), channel_id=1, source_target_pairs={{0,30},{2,0},{4,2},{6,4},{8,6},{10,8},{12,10},{14,12},{16,14},{18,... | collective-permute-start | bytes 98312 | tf_op jit(solution)/shard_map/ppermute | solution.py:19
  85.9 4.4 %collective-permute-start.14 = (bf16[128,128]{1,0:T(8,128)(2,1)S(1)}, bf16[128,128]{1,0:T(8,128)(2,1)S(1)}, u32[]{:S(2)}, u32[]{:S(2)}) collective-permute-start(bf16[128,128]{1,0:T(8,128)(2,1)S(1)} %get-tuple-element.20), channel_id=1, source_target_pairs={{0,28},{2,30},{4,0},{6,2},{8,4},{10,6},{12,8},{14,10},{16,12},{18,... | collective-permute-start | bytes 98312 | tf_op jit(solution)/shard_map/ppermute | solution.py:19
  90.4 3.3 %collective-permute-done.13 = bf16[128,128]{1,0:T(8,128)(2,1)S(1)} collective-permute-done((bf16[128,128]{1,0:T(8,128)(2,1)S(1)}, bf16[128,128]{1,0:T(8,128)(2,1)S(1)}, u32[]{:S(2)}, u32[]{:S(2)}) %collective-permute-start.13) | collective-permute-done | bytes 32800 | tf_op jit(solution)/shard_map/ppermute | solution.py:19
  93.7 3.3 %collective-permute-done.15 = bf16[128,128]{1,0:T(8,128)(2,1)S(1)} collective-permute-done((bf16[128,128]{1,0:T(8,128)(2,1)S(1)}, bf16[128,128]{1,0:T(8,128)(2,1)S(1)}, u32[]{:S(2)}, u32[]{:S(2)}) %collective-permute-start.15) | collective-permute-done | bytes 32800 | tf_op jit(solution)/shard_map/ppermute | solution.py:19
  99.2 5.0 %reduce-scatter.6.cloned.1.call-done = f32[512,128]{1,0:T(8,128)} async-done(((f32[1024,128]{1,0:T(8,128)}), f32[512,128]{1,0:T(8,128)}) %reduce-scatter.6.cloned.1.call-update) | async-done | bytes 262160 | tf_op jit(solution)/shard_map/reduce_scatter | solution.py:196
  110.5 4.0 %collective-permute-start.17 = (bf16[128,128]{1,0:T(8,128)(2,1)S(1)}, bf16[128,128]{1,0:T(8,128)(2,1)S(1)}, u32[]{:S(2)}, u32[]{:S(2)}) collective-permute-start(bf16[128,128]{1,0:T(8,128)(2,1)S(1)} %get-tuple-element.31), channel_id=1, source_target_pairs={{0,30},{2,0},{4,2},{6,4},{8,6},{10,8},{12,10},{14,12},{16,14},{18,... | collective-permute-start | bytes 98312 | tf_op jit(solution)/shard_map/ppermute | solution.py:19
  114.4 4.7 %collective-permute-start.19 = (bf16[128,128]{1,0:T(8,128)(2,1)S(1)}, bf16[128,128]{1,0:T(8,128)(2,1)S(1)}, u32[]{:S(2)}, u32[]{:S(2)}) collective-permute-start(bf16[128,128]{1,0:T(8,128)(2,1)S(1)} %get-tuple-element.29), channel_id=1, source_target_pairs={{0,28},{2,30},{4,0},{6,2},{8,4},{10,6},{12,8},{14,10},{16,12},{18,... | collective-permute-start | bytes 98312 | tf_op jit(solution)/shard_map/ppermute | solution.py:19
  121.1 11.7 %shard_map.115 = (bf16[4096,128]{1,0:T(8,128)(2,1)}, f32[1536,128]{1,0:T(8,128)S(1)}) custom-call(s32[1]{0:T(128)S(6)} %copy.38.count_ref, bf16[1536,128]{1,0:T(8,128)(2,1)S(1)} %constant_dynamic-update-slice_fusion.10.ext_ref, bf16[4096,128]{1,0:T(8,128)(2,1)S(1)} %get-tuple-element.11.latent_ref, s32[2,4096]{1,0:T(2,128)S(1)} %pad_add_fusion.ids_ref, ...), custom_call_target="tpu_custom_call" | custom-call | flops 6442450944 | bytes 2097152 | tf_op jit(solution)/shard_map/pallas_call | solution.py:135
  132.9 2.3 %collective-permute-start.20 = (bf16[128,128]{1,0:T(8,128)(2,1)S(1)}, bf16[128,128]{1,0:T(8,128)(2,1)S(1)}, u32[]{:S(2)}, u32[]{:S(2)}) collective-permute-start(bf16[128,128]{1,0:T(8,128)(2,1)S(1)} %get-tuple-element.14), channel_id=1, source_target_pairs={{0,30},{2,0},{4,2},{6,4},{8,6},{10,8},{12,10},{14,12},{16,14},{18,... | collective-permute-start | bytes 98312 | tf_op jit(solution)/shard_map/ppermute | solution.py:19
  135.1 4.5 %collective-permute-start.22 = (bf16[128,128]{1,0:T(8,128)(2,1)S(1)}, bf16[128,128]{1,0:T(8,128)(2,1)S(1)}, u32[]{:S(2)}, u32[]{:S(2)}) collective-permute-start(bf16[128,128]{1,0:T(8,128)(2,1)S(1)} %get-tuple-element.16), channel_id=1, source_target_pairs={{0,28},{2,30},{4,0},{6,2},{8,4},{10,6},{12,8},{14,10},{16,12},{18,... | collective-permute-start | bytes 98312 | tf_op jit(solution)/shard_map/ppermute | solution.py:19
  139.6 3.2 %collective-permute-done.21 = bf16[128,128]{1,0:T(8,128)(2,1)S(1)} collective-permute-done((bf16[128,128]{1,0:T(8,128)(2,1)S(1)}, bf16[128,128]{1,0:T(8,128)(2,1)S(1)}, u32[]{:S(2)}, u32[]{:S(2)}) %collective-permute-start.21) | collective-permute-done | bytes 32800 | tf_op jit(solution)/shard_map/ppermute | solution.py:19
  142.8 3.4 %collective-permute-done.23 = bf16[128,128]{1,0:T(8,128)(2,1)S(1)} collective-permute-done((bf16[128,128]{1,0:T(8,128)(2,1)S(1)}, bf16[128,128]{1,0:T(8,128)(2,1)S(1)}, u32[]{:S(2)}, u32[]{:S(2)}) %collective-permute-start.23) | collective-permute-done | bytes 32800 | tf_op jit(solution)/shard_map/ppermute | solution.py:19
  148.1 5.3 %reduce-scatter.8.cloned.1.call-done = f32[512,128]{1,0:T(8,128)} async-done(((f32[1024,128]{1,0:T(8,128)}), f32[512,128]{1,0:T(8,128)}) %reduce-scatter.8.cloned.1.call-update) | async-done | bytes 262160 | tf_op jit(solution)/shard_map/reduce_scatter | solution.py:196
  (119 shorter events, 38.8 us)
Async XLA Ops:
  7.2 48.2 %reduce-scatter.4.cloned.1.call-start = ((), (), s32[]{:S(2)}) async-start(), calls=%async_computation.3 | async-start | bytes 786432 | tf_op jit(solution)/shard_map/reduce_scatter | solution.py:196
  8.8 16.8 %collective-permute-start = (bf16[128,128]{1,0:T(8,128)(2,1)S(1)}, bf16[128,128]{1,0:T(8,128)(2,1)S(1)}, u32[]{:S(2)}, u32[]{:S(2)}) collective-permute-start(bf16[128,128]{1,0:T(8,128)(2,1)S(1)} %get-tuple-element.40), channel_id=1, source_target_pairs={{0,2},{2,4},{4,6},{6,8},{8,10},{10,12},{12,14},{14,16},{16,18},{18... | collective-permute-start | bytes 98312 | tf_op jit(solution)/shard_map/ppermute | solution.py:19
  11.8 13.8 %collective-permute-start.1 = (bf16[128,128]{1,0:T(8,128)(2,1)S(1)}, bf16[128,128]{1,0:T(8,128)(2,1)S(1)}, u32[]{:S(2)}, u32[]{:S(2)}) collective-permute-start(bf16[128,128]{1,0:T(8,128)(2,1)S(1)} %get-tuple-element.39), channel_id=1, source_target_pairs={{0,30},{2,0},{4,2},{6,4},{8,6},{10,8},{12,10},{14,12},{16,14},{18,... | collective-permute-start | bytes 98312 | tf_op jit(solution)/shard_map/ppermute | solution.py:19
  15.9 9.7 %collective-permute-start.2 = (bf16[128,128]{1,0:T(8,128)(2,1)S(1)}, bf16[128,128]{1,0:T(8,128)(2,1)S(1)}, u32[]{:S(2)}, u32[]{:S(2)}) collective-permute-start(bf16[128,128]{1,0:T(8,128)(2,1)S(1)} %get-tuple-element.38), channel_id=1, source_target_pairs={{0,4},{2,6},{4,8},{6,10},{8,12},{10,14},{12,16},{14,18},{16,20},{1... | collective-permute-start | bytes 98312 | tf_op jit(solution)/shard_map/ppermute | solution.py:19
  15.9 9.8 %collective-permute-start.3 = (bf16[128,128]{1,0:T(8,128)(2,1)S(1)}, bf16[128,128]{1,0:T(8,128)(2,1)S(1)}, u32[]{:S(2)}, u32[]{:S(2)}) collective-permute-start(bf16[128,128]{1,0:T(8,128)(2,1)S(1)} %get-tuple-element.37), channel_id=1, source_target_pairs={{0,28},{2,30},{4,0},{6,2},{8,4},{10,6},{12,8},{14,10},{16,12},{18,... | collective-permute-start | bytes 98312 | tf_op jit(solution)/shard_map/ppermute | solution.py:19
  37.1 7.6 %collective-permute-start.5 = (bf16[128,128]{1,0:T(8,128)(2,1)S(1)}, bf16[128,128]{1,0:T(8,128)(2,1)S(1)}, u32[]{:S(2)}, u32[]{:S(2)}) collective-permute-start(bf16[128,128]{1,0:T(8,128)(2,1)S(1)} %get-tuple-element.25), channel_id=1, source_target_pairs={{0,2},{2,4},{4,6},{6,8},{8,10},{10,12},{12,14},{14,16},{16,18},{18... | collective-permute-start | bytes 98312 | tf_op jit(solution)/shard_map/ppermute | solution.py:19
  40.6 6.6 %collective-permute-start.7 = (bf16[128,128]{1,0:T(8,128)(2,1)S(1)}, bf16[128,128]{1,0:T(8,128)(2,1)S(1)}, u32[]{:S(2)}, u32[]{:S(2)}) collective-permute-start(bf16[128,128]{1,0:T(8,128)(2,1)S(1)} %get-tuple-element.23), channel_id=1, source_target_pairs={{0,4},{2,6},{4,8},{6,10},{8,12},{10,14},{12,16},{14,18},{16,20},{1... | collective-permute-start | bytes 98312 | tf_op jit(solution)/shard_map/ppermute | solution.py:19
  48.9 55.3 %reduce-scatter.6.cloned.1.call-start = ((), (), s32[]{:S(2)}) async-start(), calls=%async_computation.4 | async-start | bytes 786432 | tf_op jit(solution)/shard_map/reduce_scatter | solution.py:196
  59.9 10.5 %collective-permute-start.8 = (bf16[128,128]{1,0:T(8,128)(2,1)S(1)}, bf16[128,128]{1,0:T(8,128)(2,1)S(1)}, u32[]{:S(2)}, u32[]{:S(2)}) collective-permute-start(bf16[128,128]{1,0:T(8,128)(2,1)S(1)} %get-tuple-element.36), channel_id=1, source_target_pairs={{0,2},{2,4},{4,6},{6,8},{8,10},{10,12},{12,14},{14,16},{16,18},{18... | collective-permute-start | bytes 98312 | tf_op jit(solution)/shard_map/ppermute | solution.py:19
  61.7 8.7 %collective-permute-start.9 = (bf16[128,128]{1,0:T(8,128)(2,1)S(1)}, bf16[128,128]{1,0:T(8,128)(2,1)S(1)}, u32[]{:S(2)}, u32[]{:S(2)}) collective-permute-start(bf16[128,128]{1,0:T(8,128)(2,1)S(1)} %get-tuple-element.35), channel_id=1, source_target_pairs={{0,30},{2,0},{4,2},{6,4},{8,6},{10,8},{12,10},{14,12},{16,14},{18,... | collective-permute-start | bytes 98312 | tf_op jit(solution)/shard_map/ppermute | solution.py:19
  65.6 6.6 %collective-permute-start.10 = (bf16[128,128]{1,0:T(8,128)(2,1)S(1)}, bf16[128,128]{1,0:T(8,128)(2,1)S(1)}, u32[]{:S(2)}, u32[]{:S(2)}) collective-permute-start(bf16[128,128]{1,0:T(8,128)(2,1)S(1)} %get-tuple-element.34), channel_id=1, source_target_pairs={{0,4},{2,6},{4,8},{6,10},{8,12},{10,14},{12,16},{14,18},{16,20},{1... | collective-permute-start | bytes 98312 | tf_op jit(solution)/shard_map/ppermute | solution.py:19
  65.6 6.6 %collective-permute-start.11 = (bf16[128,128]{1,0:T(8,128)(2,1)S(1)}, bf16[128,128]{1,0:T(8,128)(2,1)S(1)}, u32[]{:S(2)}, u32[]{:S(2)}) collective-permute-start(bf16[128,128]{1,0:T(8,128)(2,1)S(1)} %get-tuple-element.33), channel_id=1, source_target_pairs={{0,28},{2,30},{4,0},{6,2},{8,4},{10,6},{12,8},{14,10},{16,12},{18,... | collective-permute-start | bytes 98312 | tf_op jit(solution)/shard_map/ppermute | solution.py:19
  83.6 6.8 %collective-permute-start.12 = (bf16[128,128]{1,0:T(8,128)(2,1)S(1)}, bf16[128,128]{1,0:T(8,128)(2,1)S(1)}, u32[]{:S(2)}, u32[]{:S(2)}) collective-permute-start(bf16[128,128]{1,0:T(8,128)(2,1)S(1)} %get-tuple-element.18), channel_id=1, source_target_pairs={{0,30},{2,0},{4,2},{6,4},{8,6},{10,8},{12,10},{14,12},{16,14},{18,... | collective-permute-start | bytes 98312 | tf_op jit(solution)/shard_map/ppermute | solution.py:19
  85.9 7.8 %collective-permute-start.13 = (bf16[128,128]{1,0:T(8,128)(2,1)S(1)}, bf16[128,128]{1,0:T(8,128)(2,1)S(1)}, u32[]{:S(2)}, u32[]{:S(2)}) collective-permute-start(bf16[128,128]{1,0:T(8,128)(2,1)S(1)} %get-tuple-element.21), channel_id=1, source_target_pairs={{0,2},{2,4},{4,6},{6,8},{8,10},{10,12},{12,14},{14,16},{16,18},{18... | collective-permute-start | bytes 98312 | tf_op jit(solution)/shard_map/ppermute | solution.py:19
  85.9 7.8 %collective-permute-start.14 = (bf16[128,128]{1,0:T(8,128)(2,1)S(1)}, bf16[128,128]{1,0:T(8,128)(2,1)S(1)}, u32[]{:S(2)}, u32[]{:S(2)}) collective-permute-start(bf16[128,128]{1,0:T(8,128)(2,1)S(1)} %get-tuple-element.20), channel_id=1, source_target_pairs={{0,28},{2,30},{4,0},{6,2},{8,4},{10,6},{12,8},{14,10},{16,12},{18,... | collective-permute-start | bytes 98312 | tf_op jit(solution)/shard_map/ppermute | solution.py:19
  90.4 6.6 %collective-permute-start.15 = (bf16[128,128]{1,0:T(8,128)(2,1)S(1)}, bf16[128,128]{1,0:T(8,128)(2,1)S(1)}, u32[]{:S(2)}, u32[]{:S(2)}) collective-permute-start(bf16[128,128]{1,0:T(8,128)(2,1)S(1)} %get-tuple-element.19), channel_id=1, source_target_pairs={{0,4},{2,6},{4,8},{6,10},{8,12},{10,14},{12,16},{14,18},{16,20},{1... | collective-permute-start | bytes 98312 | tf_op jit(solution)/shard_map/ppermute | solution.py:19
  98.6 54.8 %reduce-scatter.8.cloned.1.call-start = ((), (), s32[]{:S(2)}) async-start(), calls=%async_computation.5 | async-start | bytes 786432 | tf_op jit(solution)/shard_map/reduce_scatter | solution.py:196
  108.7 10.5 %collective-permute-start.16 = (bf16[128,128]{1,0:T(8,128)(2,1)S(1)}, bf16[128,128]{1,0:T(8,128)(2,1)S(1)}, u32[]{:S(2)}, u32[]{:S(2)}) collective-permute-start(bf16[128,128]{1,0:T(8,128)(2,1)S(1)} %get-tuple-element.32), channel_id=1, source_target_pairs={{0,2},{2,4},{4,6},{6,8},{8,10},{10,12},{12,14},{14,16},{16,18},{18... | collective-permute-start | bytes 98312 | tf_op jit(solution)/shard_map/ppermute | solution.py:19
  110.5 8.7 %collective-permute-start.17 = (bf16[128,128]{1,0:T(8,128)(2,1)S(1)}, bf16[128,128]{1,0:T(8,128)(2,1)S(1)}, u32[]{:S(2)}, u32[]{:S(2)}) collective-permute-start(bf16[128,128]{1,0:T(8,128)(2,1)S(1)} %get-tuple-element.31), channel_id=1, source_target_pairs={{0,30},{2,0},{4,2},{6,4},{8,6},{10,8},{12,10},{14,12},{16,14},{18,... | collective-permute-start | bytes 98312 | tf_op jit(solution)/shard_map/ppermute | solution.py:19
  114.4 6.6 %collective-permute-start.18 = (bf16[128,128]{1,0:T(8,128)(2,1)S(1)}, bf16[128,128]{1,0:T(8,128)(2,1)S(1)}, u32[]{:S(2)}, u32[]{:S(2)}) collective-permute-start(bf16[128,128]{1,0:T(8,128)(2,1)S(1)} %get-tuple-element.30), channel_id=1, source_target_pairs={{0,4},{2,6},{4,8},{6,10},{8,12},{10,14},{12,16},{14,18},{16,20},{1... | collective-permute-start | bytes 98312 | tf_op jit(solution)/shard_map/ppermute | solution.py:19
  114.4 6.6 %collective-permute-start.19 = (bf16[128,128]{1,0:T(8,128)(2,1)S(1)}, bf16[128,128]{1,0:T(8,128)(2,1)S(1)}, u32[]{:S(2)}, u32[]{:S(2)}) collective-permute-start(bf16[128,128]{1,0:T(8,128)(2,1)S(1)} %get-tuple-element.29), channel_id=1, source_target_pairs={{0,28},{2,30},{4,0},{6,2},{8,4},{10,6},{12,8},{14,10},{16,12},{18,... | collective-permute-start | bytes 98312 | tf_op jit(solution)/shard_map/ppermute | solution.py:19
  132.9 6.8 %collective-permute-start.20 = (bf16[128,128]{1,0:T(8,128)(2,1)S(1)}, bf16[128,128]{1,0:T(8,128)(2,1)S(1)}, u32[]{:S(2)}, u32[]{:S(2)}) collective-permute-start(bf16[128,128]{1,0:T(8,128)(2,1)S(1)} %get-tuple-element.14), channel_id=1, source_target_pairs={{0,30},{2,0},{4,2},{6,4},{8,6},{10,8},{12,10},{14,12},{16,14},{18,... | collective-permute-start | bytes 98312 | tf_op jit(solution)/shard_map/ppermute | solution.py:19
  135.1 7.7 %collective-permute-start.21 = (bf16[128,128]{1,0:T(8,128)(2,1)S(1)}, bf16[128,128]{1,0:T(8,128)(2,1)S(1)}, u32[]{:S(2)}, u32[]{:S(2)}) collective-permute-start(bf16[128,128]{1,0:T(8,128)(2,1)S(1)} %get-tuple-element.17), channel_id=1, source_target_pairs={{0,2},{2,4},{4,6},{6,8},{8,10},{10,12},{12,14},{14,16},{16,18},{18... | collective-permute-start | bytes 98312 | tf_op jit(solution)/shard_map/ppermute | solution.py:19
  135.1 7.7 %collective-permute-start.22 = (bf16[128,128]{1,0:T(8,128)(2,1)S(1)}, bf16[128,128]{1,0:T(8,128)(2,1)S(1)}, u32[]{:S(2)}, u32[]{:S(2)}) collective-permute-start(bf16[128,128]{1,0:T(8,128)(2,1)S(1)} %get-tuple-element.16), channel_id=1, source_target_pairs={{0,28},{2,30},{4,0},{6,2},{8,4},{10,6},{12,8},{14,10},{16,12},{18,... | collective-permute-start | bytes 98312 | tf_op jit(solution)/shard_map/ppermute | solution.py:19
  (12 other events, 125.2 us)
Sparse Core Ops, SparseCore 0:
  49.0 6.3 reduce-scatter.3
  98.7 5.4 reduce-scatter.5
  148.0 5.3 reduce-scatter.7

commit v2 on v1

v2 whole, which is shorter than its diff:
```python
import functools

import jax
import jax.numpy as jnp
from jax import lax
from jax.experimental import pallas as pl
from jax.experimental.pallas import tpu as pltpu
from jax.sharding import PartitionSpec as P

LAYERS = 3


neighbour_offsets = (1, -1, 2, -2)
norm_floor = 0.25


def layer_norm(values):
    centre = jnp.mean(values, axis=-1, keepdims=True)
    centred = values - centre
    spread = jnp.mean(centred * centred, axis=-1, keepdims=True)
    return centred * lax.rsqrt(spread + norm_floor)


def product(first_operand, second_operand):
    return jnp.dot(first_operand, second_operand, preferred_element_type=jnp.float32)


MESH = pl.DeviceIdType.MESH
PEERS = len(neighbour_offsets)


def peer_ids(size):
    me = lax.axis_index("dom")
    return [{"dom": lax.rem(me + offset + size, size)} for offset in neighbour_offsets]


def partner_id():
    return {"tp": 1 - lax.axis_index("tp")}


def greet(size):
    barrier = pltpu.get_barrier_semaphore()
    everyone = peer_ids(size) + [partner_id()]
    for device in everyone:
        pl.semaphore_signal(barrier, inc=1, device_id=device, device_id_type=MESH)
    pl.semaphore_wait(barrier, len(everyone))


def send(source, target, sems, at, device):
    copy = pltpu.make_async_remote_copy(
        src_ref=source,
        dst_ref=target,
        send_sem=sems.at[0, at],
        recv_sem=sems.at[1, at],
        device_id=device,
        device_id_type=MESH,
    )
    copy.start()
    return copy


def fill_pick(index_ref, pick, node_total):
    slots = index_ref.shape[1]
    wanted = jnp.broadcast_to(index_ref[...], (128, slots)).T
    lane = lax.broadcasted_iota(jnp.int32, (slots, 128), 1)
    for c in range(0, node_total, 128):
        pick[:, c : c + 128] = (wanted == lane + c).astype(jnp.bfloat16)


def start_halo(size, nodes, pick, extended_ref, outgoing, incoming, sems):
    node_total = nodes.shape[0]
    slot = pick.shape[0] // PEERS
    for k in range(PEERS):
        outgoing[k] = product(pick[k * slot : (k + 1) * slot, :], nodes).astype(jnp.bfloat16)
    extended_ref[:node_total, :] = nodes
    peers = peer_ids(size)
    return [send(outgoing.at[k], incoming.at[k], sems, k, peers[k]) for k in range(PEERS)]


def finish_halo(copies, extended_ref, incoming):
    slot = incoming.shape[1]
    first = extended_ref.shape[0] - PEERS * slot
    for k, copy in enumerate(copies):
        copy.wait()
        extended_ref[first + k * slot : first + (k + 1) * slot, :] = incoming[k]


def start_kernel(size, *refs):
    nodes_ref, index_ref = refs[:2]
    halves = refs[2:6]
    extended_ref = refs[6]
    fulls = refs[7:11]
    others = refs[11:15]
    outgoing, incoming, pick, halo_sems, weight_sems = refs[15:]
    greet(size)
    weight_copies = [
        send(half, other, weight_sems, i, partner_id())
        for i, (half, other) in enumerate(zip(halves, others))
    ]
    fill_pick(index_ref, pick, nodes_ref.shape[0])
    copies = start_halo(size, nodes_ref[...], pick, extended_ref, outgoing, incoming, halo_sems)
    mine = lax.axis_index("tp")
    for half, other, full, copy in zip(halves, others, fulls, weight_copies):
        copy.wait()
        layers, rows, columns = half.shape
        for layer in range(layers):
            if columns < full.shape[2]:
                shape = (columns, full.shape[2])
                gap = lax.broadcasted_iota(jnp.int32, shape, 1)
                gap = gap - lax.broadcasted_iota(jnp.int32, shape, 0)
                own_place = (gap == mine * columns).astype(jnp.bfloat16)
                far_place = (gap == (1 - mine) * columns).astype(jnp.bfloat16)
                joined = product(half[layer], own_place) + product(other[layer], far_place)
                full[layer] = joined.astype(jnp.bfloat16)
            else:
                near, far = half[layer], other[layer]
                full[layer, :rows, :] = jnp.where(mine == 0, near, far)
                full[layer, rows:, :] = jnp.where(mine == 0, far, near)
    finish_halo(copies, extended_ref, incoming)


def node_kernel(size, more, *refs):
    extended_ref, own_ref, back_ref, index_ref, win_ref, wout_ref, result_ref = refs[:7]
    own_far, back_near, back_far, sums_sems, table = refs[7:12]
    node_total, width = own_ref.shape
    slots = index_ref.shape[1]
    slot = slots // PEERS
    peers = peer_ids(size)
    opposite = [neighbour_offsets.index(-offset) for offset in neighbour_offsets]
    greet(size)
    own_copy = send(own_ref, own_far, sums_sems, 0, partner_id())
    back_copies = [
        send(
            back_ref.at[pl.ds(k * slot, slot), :], back_near.at[pl.ds(k * slot, slot), :],
            sums_sems, 1 + k, peers[opposite[k]],
        )
        for k in range(PEERS)
    ]
    wanted = jnp.broadcast_to(index_ref[...], (128, slots))
    row = lax.broadcasted_iota(jnp.int32, (128, slots), 0)
    for c in range(0, node_total, 128):
        table[c : c + 128, :] = (wanted == row + c).astype(jnp.bfloat16)
    if more:
        outgoing, incoming, pick, halo_sems = refs[12:]
        fill_pick(index_ref, pick, node_total)
    nodes = extended_ref[:node_total, :]
    linear = product(nodes, win_ref[:width, :])
    far_copies = []
    for k in range(PEERS):
        back_copies[k].wait()
        rows = pl.ds(k * slot, slot)
        far_copies.append(
            send(back_near.at[rows, :], back_far.at[rows, :], sums_sems, 1 + PEERS + k, partner_id())
        )
    arrived = product(table[...], back_near[...])
    own_copy.wait()
    owned = own_ref[...] + own_far[...]
    for copy in far_copies:
        copy.wait()
    owned = owned + (arrived + product(table[...], back_far[...]))
    linear = linear + product(owned.astype(jnp.bfloat16), win_ref[width:, :])
    hidden = jnp.maximum(linear, 0.0).astype(jnp.bfloat16)
    update = layer_norm(product(hidden, wout_ref[...]))
    nodes = (nodes.astype(jnp.float32) + update).astype(jnp.bfloat16)
    if more:
        copies = start_halo(size, nodes, pick, result_ref, outgoing, incoming, halo_sems)
        finish_halo(copies, result_ref, incoming)
    else:
        result_ref[...] = nodes


def halo_scratch(node_total, slots, width):
    return [
        pltpu.VMEM((PEERS, slots // PEERS, width), jnp.bfloat16),
        pltpu.VMEM((PEERS, slots // PEERS, width), jnp.bfloat16),
        pltpu.VMEM((slots, node_total), jnp.bfloat16),
        pltpu.SemaphoreType.DMA((2, PEERS)),
    ]


def start_stage(nodes, index_row, halves):
    node_total, width = nodes.shape
    slots = index_row.shape[1]
    whole = pl.BlockSpec(memory_space=pltpu.VMEM)
    parts = lax.axis_size("tp")
    fulls = []
    for axis, half in zip((2, 1, 2, 1), halves):
        shape = list(half.shape)
        shape[axis] *= parts
        fulls.append(jax.ShapeDtypeStruct(tuple(shape), half.dtype))
    extended = jax.ShapeDtypeStruct((node_total + slots, width), nodes.dtype)
    return pl.pallas_call(
        functools.partial(start_kernel, lax.axis_size("dom")),
        out_shape=(extended, *fulls),
        in_specs=[whole] * 6,
        out_specs=(whole,) * 5,
        scratch_shapes=[pltpu.VMEM(half.shape, half.dtype) for half in halves]
        + halo_scratch(node_total, slots, width)
        + [pltpu.SemaphoreType.DMA((2, 4))],
        compiler_params=pltpu.CompilerParams(
            collective_id=0, has_side_effects=True, vmem_limit_bytes=40 * 1024 * 1024
        ),
    )(nodes, index_row, *halves)


def node_stage(more, extended, own, back, index_row, weight_in, weight_out):
    node_total, width = own.shape
    slots = index_row.shape[1]
    whole = pl.BlockSpec(memory_space=pltpu.VMEM)
    rows = node_total + slots if more else node_total
    scratch = [
        pltpu.VMEM((node_total, width), jnp.float32),
        pltpu.VMEM((slots, width), jnp.bfloat16),
        pltpu.VMEM((slots, width), jnp.bfloat16),
        pltpu.SemaphoreType.DMA((2, 1 + 2 * PEERS)),
        pltpu.VMEM((node_total, slots), jnp.bfloat16),
    ]
    if more:
        scratch = scratch + halo_scratch(node_total, slots, width)
    return pl.pallas_call(
        functools.partial(node_kernel, lax.axis_size("dom"), more),
        out_shape=jax.ShapeDtypeStruct((rows, width), extended.dtype),
        in_specs=[whole] * 6,
        out_specs=whole,
        scratch_shapes=scratch,
        compiler_params=pltpu.CompilerParams(
            collective_id=1 if more else 2,
            has_side_effects=True,
            vmem_limit_bytes=40 * 1024 * 1024,
        ),
    )(extended, own, back, index_row, weight_in, weight_out)


LOW = 256
BLOCK = 1024


def edge_kernel(
    count_ref, ext_ref, latent_ref, ids_ref, win_ref, wout_ref, renewed_ref, own_ref, back_ref,
    send_table, recv_table, sums,
):
    width = ext_ref.shape[1]
    high = ext_ref.shape[0] // LOW
    rows = latent_ref.shape[0]
    block = min(BLOCK, rows)
    for h in range(high):
        part = ext_ref[h * LOW : (h + 1) * LOW, :]
        lanes = slice(h * width, (h + 1) * width)
        send_table[:, lanes] = product(part, win_ref[width : 2 * width, :]).astype(jnp.bfloat16)
        recv_table[:, lanes] = product(part, win_ref[2 * width :, :]).astype(jnp.bfloat16)
    sums[...] = jnp.zeros_like(sums)
    weight_out = wout_ref[...]
    count = count_ref[0]

    def gathered(ids, table):
        low = ids & (LOW - 1)
        lane = lax.broadcasted_iota(jnp.int32, (block, width), 1)
        halves = [(low == lane + c).astype(jnp.bfloat16) for c in range(0, LOW, width)]
        all_rows = product(jnp.concatenate(halves, axis=1), table[...])
        top = ids // LOW
        found = all_rows[:, :width]
        for h in range(1, high):
            found = jnp.where(top == h, all_rows[:, h * width : (h + 1) * width], found)
        return found

    def step(i, carry):
        at = pl.ds(pl.multiple_of(i * block, block), block)
        send_row = ids_ref[0:1, at]
        recv_row = ids_ref[1:2, at]
        send_ids = jnp.broadcast_to(send_row, (width, block)).T
        recv_ids = jnp.broadcast_to(recv_row, (width, block)).T
        latent = latent_ref[at, :]
        linear = product(latent, win_ref[:width, :])
        linear = linear + gathered(send_ids, send_table) + gathered(recv_ids, recv_table)
        hidden = jnp.maximum(linear, 0.0).astype(jnp.bfloat16)
        message = layer_norm(product(hidden, weight_out))
        position = lax.broadcasted_iota(jnp.int32, (block, width), 0) + i * block
        message = jnp.where(position < count, message, 0.0).astype(jnp.bfloat16)
        wide = message.astype(jnp.float32)
        renewed_ref[at, :] = (latent.astype(jnp.float32) + wide).astype(jnp.bfloat16)
        top = recv_ids // LOW
        spread = jnp.concatenate(
            [jnp.where(top == h, wide, 0.0).astype(jnp.bfloat16) for h in range(high)], axis=1
        )
        low_row = jnp.broadcast_to(recv_row & (LOW - 1), (LOW, block))
        table = (low_row == lax.broadcasted_iota(jnp.int32, (LOW, block), 0)).astype(jnp.bfloat16)
        sums[...] += product(table, spread)
        return carry

    lax.fori_loop(0, rows // block, step, 0)
    for h in range(high):
        part = sums[:, h * width : (h + 1) * width]
        at = h * LOW
        if at < own_ref.shape[0]:
            own_ref[at : at + LOW, :] = part
        else:
            at = at - own_ref.shape[0]
            back_ref[at : at + LOW, :] = part.astype(jnp.bfloat16)


def edge_stage(node_total, extended, edges_now, id_rows, edge_count, weight_in, weight_out):
    total, width = extended.shape
    rows = edges_now.shape[0]
    high = total // LOW
    whole = pl.BlockSpec(memory_space=pltpu.VMEM)
    return pl.pallas_call(
        edge_kernel,
        out_shape=(
            jax.ShapeDtypeStruct((rows, width), jnp.bfloat16),
            jax.ShapeDtypeStruct((node_total, width), jnp.float32),
            jax.ShapeDtypeStruct((total - node_total, width), jnp.bfloat16),
        ),
        in_specs=[pl.BlockSpec(memory_space=pltpu.SMEM)] + [whole] * 5,
        out_specs=(whole, whole, whole),
        scratch_shapes=[
            pltpu.VMEM((LOW, high * width), jnp.bfloat16),
            pltpu.VMEM((LOW, high * width), jnp.bfloat16),
            pltpu.VMEM((LOW, high * width), jnp.float32),
        ],
        compiler_params=pltpu.CompilerParams(vmem_limit_bytes=48 * 1024 * 1024),
        cost_estimate=pl.CostEstimate(
            flops=8 * rows * total * width, bytes_accessed=4 * rows * width, transcendentals=rows
        ),
    )(edge_count, extended, edges_now, id_rows, weight_in, weight_out)


def local(
    node_latent,
    edge_latent,
    edge_sender,
    edge_receiver,
    edge_count,
    send_index,
    edge_in,
    edge_out,
    node_in,
    node_out,
):
    node_total = node_latent.shape[0]
    index_row = send_index.reshape(1, -1)
    id_rows = jnp.stack([edge_sender, edge_receiver])
    current, full_in, full_out, node_first, node_second = start_stage(
        node_latent, index_row, (edge_in, edge_out, node_in, node_out)
    )
    edges_now = edge_latent
    for layer in range(LAYERS):
        edges_now, own, back = edge_stage(
            node_total, current, edges_now, id_rows, edge_count, full_in[layer], full_out[layer]
        )
        more = layer + 1 < LAYERS
        current = node_stage(
            more, current, own, back, index_row, node_first[layer], node_second[layer]
        )
    return (current, edges_now)


def solution(mesh):
    return jax.shard_map(
        local,
        mesh=mesh,
        in_specs=(
            P("dom", None),
            P(("dom", "tp"), None),
            P(("dom", "tp")),
            P(("dom", "tp")),
            P(("dom", "tp")),
            P("dom", None, None),
            P(None, None, "tp"),
            P(None, "tp", None),
            P(None, None, "tp"),
            P(None, "tp", None),
        ),
        out_specs=(P("dom", None), P(("dom", "tp"), None)),
        check_vma=False,
    )
```

time: 165 us -> 91.6 us (0.56)
  Pallas kernels: 34.2 us -> 86.2 us
  starting transfers between devices: 50.7 us -> 0 us
  waiting for transfers between devices: 35.8 us -> 0 us
  blocking collectives: 13.8 us -> 0 us
  between operations: 14.9 us -> 1.42 us
  matrix products: 11.9 us -> 0 us
    pallas_call x0 -> x4, Pallas kernels: none -> 51.9 us  [the longest x3 41.3 us: node_stage(): pl.pallas_call(functools.partial(node_kernel, lax.axis_size('dom'), more)...]
    ppermute x24 -> x0, starting transfers between devices: 50.4 us -> none  [from_behind(): lax.ppermute(array, axis, [(i, (i + by) % length) for i in range(length)])]
    ppermute x24 -> x0, waiting for transfers between devices: 23.1 us -> none  [from_behind(): lax.ppermute(array, axis, [(i, (i + by) % length) for i in range(length)])]
    all_gather x7 -> x0, blocking collectives: 13.8 us -> none  [the longest x3 5.98 us: local(): nodes_now = lax.all_gather(renewed, 'tp', axis=0, tiled=True)]
    reduce_scatter x3 -> x0, waiting for transfers between devices: 12.7 us -> none  [local(): lax.psum_scatter(owned_sums, 'tp', scatter_dimension=0, tiled=True)]
    dot_general x12 -> x0, matrix products: 11.9 us -> none  [the longest x9 7.1 us: product(): jnp.dot(first_operand, second_operand, preferred_element_type=jnp.float32)]
  transfers between devices with their start and end apart: 27 -> 0, of which waited for: 11 -> 0; matrix products, arithmetic and copies ran while one was open for 1% -> 0% of each run, Pallas kernels for 0% -> 0%
where the time goes in v2:
time: 91.6 us; the launch traced here: 91.2 us
  Pallas kernels  86.2 us (94%)
  local copies, waits for them, and re-layouts  2.79 us (3%)
  between operations  1.42 us (2%)
    pallas_call x3, Pallas kernels, node_stage(): pl.pallas_call(functools.partial(node_kernel, lax.axis_size('dom'), more)...  41.3 us
    pallas_call x3, Pallas kernels, edge_stage(): pl.pallas_call(edge_kernel, out_shape=(jax.ShapeDtypeStruct((rows, width)...  34.4 us
    pallas_call x1, Pallas kernels, start_stage(): pl.pallas_call(functools.partial(start_kernel, lax.axis_size('dom')), out...  10.6 us
    unnamed x15, local copies, waits for them, and re-layouts  2.74 us

profile of v2, /device:TPU:0, one launch (start us, length us, event | category | flops | bytes accessed | tf_op | source)
XLA Modules:
  0.0 91.2 jit_solution(861535812683451063)
XLA Ops:
  1.3 0.8 pad_add_fusion.ids_ref
  2.0 0.0 copy-start.5
  2.1 1.1 %copy.13.refs_4_ = bf16[3,256,64]{2,1,0:T(8,128)(2,1)S(1)} copy(bf16[3,256,64]{1,2,0:T(8,128)(2,1)} %param.18) | data formatting | bytes 196608 | tf_op args[8]
  3.2 0.0 copy-done.5
  3.2 0.0 copy-start
  3.2 0.0 copy-start.1
  3.2 0.0 copy-start.2
  3.2 0.0 copy-start.3
  3.2 0.2 copy.12.refs_2_
  3.4 0.7 copy-done
  4.1 0.0 copy-done.1
  4.1 0.0 copy-done.2
  4.1 0.0 copy-done.3
  4.1 0.0 copy-start.4
  4.1 10.6 %shard_map.113 = (bf16[1536,128]{1,0:T(8,128)(2,1)S(1)}, bf16[3,384,128]{2,1,0:T(8,128)(2,1)S(1)}, bf16[3,128,128]{2,1,0:T(8,128)(2,1)S(1)}, bf16[3,256,128]{2,1,0:T(8,128)(2,1)S(1)}, bf16[3,128,128]{2,1,0:T(8,128)(2,1)S(1)}) custom-call(bf16[1024,128]{1,0:T(8,128)(2,1)S(1)} %copy-done, s32[1,512]{1,0:T(1,128)S(1)} %bitcast.27, ...), custom_call_target="tpu_custom_call" | custom-call | tf_op jit(solution)/shard_map/pallas_call | solution.py:192
  14.8 0.0 copy-done.4
  14.8 11.2 %shard_map.114 = (bf16[4096,128]{1,0:T(8,128)(2,1)S(1)}, f32[1024,128]{1,0:T(8,128)S(1)}, bf16[512,128]{1,0:T(8,128)(2,1)S(1)}) custom-call(s32[1]{0:T(128)S(6)} %copy.15.count_ref, bf16[1536,128]{1,0:T(8,128)(2,1)S(1)} %get-tuple-element.16.ext_ref.refs_0_, bf16[4096,128]{1,0:T(8,128)(2,1)S(1)} %copy-done.4, s32[2,4096]{1,0:T(2,128)S(1)} %pad_add_fusion.ids_ref, ...), custom_call_target="tpu_custom_call" | custom-call | flops 6442450944 | bytes 2097152 | tf_op jit(solution)/shard_map/pallas_call | solution.py:306
  26.0 17.4 %shard_map.115.ext_ref.refs_0_ = bf16[1536,128]{1,0:T(8,128)(2,1)S(1)} custom-call(bf16[1536,128]{1,0:T(8,128)(2,1)S(1)} %get-tuple-element.16.ext_ref.refs_0_, f32[1024,128]{1,0:T(8,128)S(1)} %get-tuple-element.19.refs_1_, bf16[512,128]{1,0:T(8,128)(2,1)S(1)} %get-tuple-element.20.refs_2_, s32[1,512]{1,0:T(1,128)S(1)} %bitcast.28, ...), custom_call_target="tpu_custom_call" | custom-call | tf_op jit(solution)/shard_map/pallas_call | solution.py:220
  43.5 11.2 %shard_map.116 = (bf16[4096,128]{1,0:T(8,128)(2,1)S(1)}, f32[1024,128]{1,0:T(8,128)S(1)}, bf16[512,128]{1,0:T(8,128)(2,1)S(1)}) custom-call(s32[1]{0:T(128)S(6)} %copy.15.count_ref, bf16[1536,128]{1,0:T(8,128)(2,1)S(1)} %shard_map.115.ext_ref.refs_0_, bf16[4096,128]{1,0:T(8,128)(2,1)S(1)} %get-tuple-element.23.latent_ref, ...), custom_call_target="tpu_custom_call" | custom-call | flops 6442450944 | bytes 2097152 | tf_op jit(solution)/shard_map/pallas_call | solution.py:306
  54.7 13.9 %shard_map.117.ext_ref.refs_0_ = bf16[1536,128]{1,0:T(8,128)(2,1)S(1)} custom-call(bf16[1536,128]{1,0:T(8,128)(2,1)S(1)} %shard_map.115.ext_ref.refs_0_, f32[1024,128]{1,0:T(8,128)S(1)} %get-tuple-element.24.refs_1_, bf16[512,128]{1,0:T(8,128)(2,1)S(1)} %get-tuple-element.25.refs_2_, s32[1,512]{1,0:T(1,128)S(1)} %bitcast.29, ...), custom_call_target="tpu_custom_call" | custom-call | tf_op jit(solution)/shard_map/pallas_call | solution.py:220
  68.6 11.9 %shard_map.118 = (bf16[4096,128]{1,0:T(8,128)(2,1)}, f32[1024,128]{1,0:T(8,128)S(1)}, bf16[512,128]{1,0:T(8,128)(2,1)S(1)}) custom-call(s32[1]{0:T(128)S(6)} %copy.15.count_ref, bf16[1536,128]{1,0:T(8,128)(2,1)S(1)} %shard_map.117.ext_ref.refs_0_, bf16[4096,128]{1,0:T(8,128)(2,1)S(1)} %get-tuple-element.26.latent_ref, s32[2,4096]{1,0:T(2,128)S(1)} %pad_add_fusion.ids_ref, ...), custom_call_target="tpu_custom_call" | custom-call | flops 6442450944 | bytes 2097152 | tf_op jit(solution)/shard_map/pallas_call | solution.py:306
  80.5 10.0 %shard_map.119 = bf16[1024,128]{1,0:T(8,128)(2,1)S(1)} custom-call(bf16[1536,128]{1,0:T(8,128)(2,1)S(1)} %shard_map.117.ext_ref.refs_0_, f32[1024,128]{1,0:T(8,128)S(1)} %get-tuple-element.27.refs_1_, bf16[512,128]{1,0:T(8,128)(2,1)S(1)} %get-tuple-element.28.refs_2_, s32[1,512]{1,0:T(1,128)S(1)} %bitcast.30, ...), custom_call_target="tpu_custom_call" | custom-call | tf_op jit(solution)/shard_map/pallas_call | solution.py:220
  90.5 0.7 copy.16
  (3 shorter events, 0.1 us)
Async XLA Ops:
  2.0 1.1 %copy-start.5 = (bf16[3,384,64]{1,2,0:T(8,128)(2,1)S(1)}, bf16[3,384,64]{1,2,0:T(8,128)(2,1)}, u32[]{:S(2)}) copy-start(bf16[3,384,64]{1,2,0:T(8,128)(2,1)} %param.16) | copy-start | bytes 442372
  3.2 1.0 %copy-start = (bf16[1024,128]{1,0:T(8,128)(2,1)S(1)}, bf16[1024,128]{1,0:T(8,128)(2,1)}, u32[]{:S(2)}) copy-start(bf16[1024,128]{1,0:T(8,128)(2,1)} %refs_0_.1) | copy-start | bytes 786436
  3.2 0.9 %copy-start.1 = (bf16[3,64,128]{2,1,0:T(8,128)(2,1)S(1)}, bf16[3,64,128]{2,1,0:T(8,128)(2,1)}, u32[]{:S(2)}) copy-start(bf16[3,64,128]{2,1,0:T(8,128)(2,1)} %refs_3_.1) | copy-start | bytes 147460
  3.2 0.9 %copy-start.2 = (bf16[3,64,128]{2,1,0:T(8,128)(2,1)S(1)}, bf16[3,64,128]{2,1,0:T(8,128)(2,1)}, u32[]{:S(2)}) copy-start(bf16[3,64,128]{2,1,0:T(8,128)(2,1)} %refs_5_.1) | copy-start | bytes 147460
  3.2 0.9 %copy-start.3 = (s32[1,4,128]{2,1,0:T(4,128)S(1)}, s32[1,4,128]{2,1,0:T(4,128)}, u32[]{:S(2)}) copy-start(s32[1,4,128]{2,1,0:T(4,128)} %param.15) | copy-start | bytes 6148
  4.1 10.7 %copy-start.4 = (bf16[4096,128]{1,0:T(8,128)(2,1)S(1)}, bf16[4096,128]{1,0:T(8,128)(2,1)}, u32[]{:S(2)}) copy-start(bf16[4096,128]{1,0:T(8,128)(2,1)} %latent_ref.1) | copy-start | bytes 3145732

commit v3 on v0

v3 whole, which is shorter than its diff:
```python
import functools

import jax
import jax.numpy as jnp
from jax import lax
from jax.experimental import pallas as pl
from jax.experimental.pallas import tpu as pltpu
from jax.sharding import PartitionSpec as P

LAYERS = 3


neighbour_offsets = (1, -1, 2, -2)
norm_floor = 0.25


def layer_norm(values):
    centre = jnp.mean(values, axis=-1, keepdims=True)
    centred = values - centre
    spread = jnp.mean(centred * centred, axis=-1, keepdims=True)
    return centred * lax.rsqrt(spread + norm_floor)


def product(first_operand, second_operand):
    return jnp.dot(first_operand, second_operand, preferred_element_type=jnp.float32)


MESH = pl.DeviceIdType.MESH
PEERS = len(neighbour_offsets)


def peer_ids(size):
    me = lax.axis_index("dom")
    return [{"dom": lax.rem(me + offset + size, size)} for offset in neighbour_offsets]


def partner_id():
    return {"tp": 1 - lax.axis_index("tp")}


def greet(size):
    barrier = pltpu.get_barrier_semaphore()
    everyone = peer_ids(size) + [partner_id()]
    for device in everyone:
        pl.semaphore_signal(barrier, inc=1, device_id=device, device_id_type=MESH)
    pl.semaphore_wait(barrier, len(everyone))


def send(source, target, sems, at, device):
    copy = pltpu.make_async_remote_copy(
        src_ref=source,
        dst_ref=target,
        send_sem=sems.at[0, at],
        recv_sem=sems.at[1, at],
        device_id=device,
        device_id_type=MESH,
    )
    copy.start()
    return copy


def fill_pick(index_ref, pick, node_total):
    slots = index_ref.shape[1]
    wanted = jnp.broadcast_to(index_ref[...], (128, slots)).T
    lane = lax.broadcasted_iota(jnp.int32, (slots, 128), 1)
    for c in range(0, node_total, 128):
        pick[:, c : c + 128] = (wanted == lane + c).astype(jnp.bfloat16)


def join_halves(mine, half, other, full):
    layers, rows, columns = half.shape
    for layer in range(layers):
        if columns < full.shape[2]:
            shape = (columns, full.shape[2])
            gap = lax.broadcasted_iota(jnp.int32, shape, 1)
            gap = gap - lax.broadcasted_iota(jnp.int32, shape, 0)
            own_place = (gap == mine * columns).astype(jnp.bfloat16)
            far_place = (gap == (1 - mine) * columns).astype(jnp.bfloat16)
            joined = product(half[layer], own_place) + product(other[layer], far_place)
            full[layer] = joined.astype(jnp.bfloat16)
        else:
            near, far = half[layer], other[layer]
            full[layer, :rows, :] = jnp.where(mine == 0, near, far)
            full[layer, rows:, :] = jnp.where(mine == 0, far, near)


LOW = 256
BLOCK = 1024


def kernel(size, *refs):
    count_ref, nodes_in, latent_ref, sender_ref, receiver_ref, index_ref = refs[:6]
    halves, refs = refs[6:10], refs[10:]
    nodes_ref, edges_ref = refs[:2]
    others, fulls, refs = refs[2:6], refs[6:10], refs[10:]
    outgoing, halo_in, back_out, back_near, back_far, own_sums, own_far = refs[:7]
    pick, place, low_hot, tops, recv_hot, linear, messages = refs[7:14]
    send_table, recv_table, back_sums, sems, weight_sems = refs[14:]
    edge_in, edge_out, node_in, node_out = fulls
    node_total, width = nodes_ref.shape
    rows = edges_ref.shape[0]
    slots = index_ref.shape[1]
    slot = slots // PEERS
    own_high, high = node_total // LOW, (node_total + slots) // LOW
    block = min(BLOCK, rows)
    peers = peer_ids(size)
    opposite = [neighbour_offsets.index(-offset) for offset in neighbour_offsets]
    partner = partner_id()
    mine = lax.axis_index("tp")
    per_layer = 2 + 3 * PEERS
    own_group = own_high // 2

    def each_block(body):
        def step(i, carry):
            body(pl.multiple_of(i * block, block))
            return carry

        lax.fori_loop(0, rows // block, step, 0)

    def send_halo(layer, nodes):
        base = layer * per_layer
        for k in range(PEERS):
            part = product(pick[k * slot : (k + 1) * slot, :], nodes)
            outgoing[layer, k * slot : (k + 1) * slot, :] = part.astype(jnp.bfloat16)
        nodes_ref[...] = nodes
        copies = []
        for k in range(PEERS):
            at = pl.ds(k * slot, slot)
            copies.append(
                send(outgoing.at[layer, at], halo_in.at[layer, at], sems, base + k, peers[k])
            )
        return copies

    def fill_tables(layer, part, h):
        lanes = slice(h * width, (h + 1) * width)
        weight = edge_in[layer]
        send_table[:, lanes] = product(part, weight[width : 2 * width, :]).astype(jnp.bfloat16)
        recv_table[:, lanes] = product(part, weight[2 * width :, :]).astype(jnp.bfloat16)

    def gathered(side, at, table, first, last):
        found_rows = product(
            low_hot[side, pl.ds(at, block), :], table[:, first * width : last * width]
        )
        top = tops[side, pl.ds(at, block), :]
        found = jnp.zeros((block, width), jnp.float32)
        for h in range(first, last):
            lanes = slice((h - first) * width, (h - first + 1) * width)
            found = jnp.where(top == h, found_rows[:, lanes], found)
        return found

    def scattered(at, message, first, last):
        wide = message.astype(jnp.float32)
        top = tops[1, pl.ds(at, block), :]
        spread = [
            jnp.where(top == h, wide, 0.0).astype(jnp.bfloat16) for h in range(first, last)
        ]
        return product(recv_hot[:, pl.ds(at, block)], jnp.concatenate(spread, axis=1))

    greet(size)
    weight_copies = [
        send(half, other, weight_sems, i, partner)
        for i, (half, other) in enumerate(zip(halves, others))
    ]
    fill_pick(index_ref, pick, node_total)
    halo_copies = send_halo(0, nodes_in[...])
    wanted = jnp.broadcast_to(index_ref[...], (128, slots))
    row = lax.broadcasted_iota(jnp.int32, (128, slots), 0)
    for c in range(0, node_total, 128):
        place[c : c + 128, :] = (wanted == row + c).astype(jnp.bfloat16)
    for half, other, full, copy in zip(halves, others, fulls, weight_copies):
        copy.wait()
        join_halves(mine, half, other, full)

    def prepare(at):
        here = pl.ds(at, block)
        for side, ids_ref in enumerate((sender_ref, receiver_ref)):
            ids = jnp.broadcast_to(ids_ref[0:1, here], (width, block)).T
            low = ids & (LOW - 1)
            lane = lax.broadcasted_iota(jnp.int32, (block, width), 1)
            for c in range(0, LOW, width):
                low_hot[side, here, c : c + width] = (low == lane + c).astype(jnp.bfloat16)
            tops[side, here, :] = ids // LOW
        low_row = jnp.broadcast_to(receiver_ref[0:1, here] & (LOW - 1), (LOW, block))
        down = lax.broadcasted_iota(jnp.int32, (LOW, block), 0)
        recv_hot[:, here] = (low_row == down).astype(jnp.bfloat16)
        linear[here, :] = product(latent_ref[here, :], edge_in[0, :width, :])

    each_block(prepare)
    for layer in range(LAYERS):
        base = layer * per_layer
        more = layer + 1 < LAYERS
        latents = latent_ref if layer == 0 else edges_ref
        for h in range(own_high):
            fill_tables(layer, nodes_ref[h * LOW : (h + 1) * LOW, :], h)

        def own_gather(at):
            here = pl.ds(at, block)
            found = gathered(0, at, send_table, 0, own_high)
            linear[here, :] += found + gathered(1, at, recv_table, 0, own_high)

        each_block(own_gather)
        for copy in halo_copies:
            copy.wait()
        for h in range(own_high, high):
            at = (h - own_high) * LOW
            fill_tables(layer, halo_in[layer, at : at + LOW, :], h)
        back_sums[...] = jnp.zeros_like(back_sums)

        def finish_edges(at):
            here = pl.ds(at, block)
            found = linear[here, :] + gathered(0, at, send_table, own_high, high)
            found = found + gathered(1, at, recv_table, own_high, high)
            hidden = jnp.maximum(found, 0.0).astype(jnp.bfloat16)
            message = layer_norm(product(hidden, edge_out[layer]))
            position = lax.broadcasted_iota(jnp.int32, (block, width), 0) + at
            message = jnp.where(position < count_ref[0], message, 0.0).astype(jnp.bfloat16)
            messages[here, :] = message
            renewed = latents[here, :].astype(jnp.float32) + message.astype(jnp.float32)
            edges_ref[here, :] = renewed.astype(jnp.bfloat16)
            back_sums[...] += scattered(at, message, own_high, high)

        each_block(finish_edges)
        for h in range(own_high, high):
            at = (h - own_high) * LOW
            lanes = slice(at // LOW * width, (at // LOW + 1) * width)
            back_out[layer, at : at + LOW, :] = back_sums[:, lanes].astype(jnp.bfloat16)
        own_sums[layer] = jnp.zeros(own_sums.shape[1:], jnp.float32)
        back_copies = []
        for k in range(PEERS):
            at = pl.ds(k * slot, slot)
            back_copies.append(
                send(
                    back_out.at[layer, at], back_near.at[layer, at],
                    sems, base + PEERS + k, peers[opposite[k]],
                )
            )
        own_copies = []
        for group in range(2):
            first = group * own_group

            def own_scatter(at):
                message = messages[pl.ds(at, block), :]
                own_sums[layer, group] += scattered(at, message, first, first + own_group)

            each_block(own_scatter)
            own_copies.append(
                send(
                    own_sums.at[layer, group], own_far.at[layer, group],
                    sems, base + 3 * PEERS + group, partner,
                )
            )
        far_copies = []
        for k in range(PEERS):
            back_copies[k].wait()
            at = pl.ds(k * slot, slot)
            far_copies.append(
                send(
                    back_near.at[layer, at], back_far.at[layer, at],
                    sems, base + 2 * PEERS + k, partner,
                )
            )
        if more:

            def next_linear(at):
                here = pl.ds(at, block)
                linear[here, :] = product(edges_ref[here, :], edge_in[layer + 1, :width, :])

            each_block(next_linear)
        nodes = nodes_ref[...]
        arrived = product(place[...], back_near[layer])
        weight = node_in[layer]
        hidden = product(nodes, weight[:width, :])
        for copy in own_copies:
            copy.wait()
        owned = []
        for h in range(own_high):
            group, at = h // own_group, (h % own_group) * width
            near = own_sums[layer, group, :, at : at + width]
            owned.append(near + own_far[layer, group, :, at : at + width])
        for copy in far_copies:
            copy.wait()
        arrived = arrived + product(place[...], back_far[layer])
        aggregate = (jnp.concatenate(owned, axis=0) + arrived).astype(jnp.bfloat16)
        hidden = hidden + product(aggregate, weight[width:, :])
        hidden = jnp.maximum(hidden, 0.0).astype(jnp.bfloat16)
        update = layer_norm(product(hidden, node_out[layer]))
        nodes = (nodes.astype(jnp.float32) + update).astype(jnp.bfloat16)
        if more:
            halo_copies = send_halo(layer + 1, nodes)
        else:
            nodes_ref[...] = nodes


def local(
    node_latent,
    edge_latent,
    edge_sender,
    edge_receiver,
    edge_count,
    send_index,
    edge_in,
    edge_out,
    node_in,
    node_out,
):
    node_total, width = node_latent.shape
    rows = edge_latent.shape[0]
    index_row = send_index.reshape(1, -1)
    slots = index_row.shape[1]
    parts = lax.axis_size("tp")
    halves = (edge_in, edge_out, node_in, node_out)
    fulls = []
    for axis, half in zip((2, 1, 2, 1), halves):
        shape = list(half.shape)
        shape[axis] *= parts
        fulls.append(tuple(shape))
    narrow, total = jnp.bfloat16, node_total + slots
    own_group = (LAYERS, 2, LOW, node_total // LOW // 2 * width)
    scratch = [pltpu.VMEM(half.shape, half.dtype) for half in halves]
    scratch += [pltpu.VMEM(shape, narrow) for shape in fulls]
    scratch += [pltpu.VMEM((LAYERS, slots, width), narrow) for _ in range(5)]
    scratch += [
        pltpu.VMEM(own_group, jnp.float32),
        pltpu.VMEM(own_group, jnp.float32),
        pltpu.VMEM((slots, node_total), narrow),
        pltpu.VMEM((node_total, slots), narrow),
        pltpu.VMEM((2, rows, LOW), narrow),
        pltpu.VMEM((2, rows, width), jnp.int32),
        pltpu.VMEM((LOW, rows), narrow),
        pltpu.VMEM((rows, width), jnp.float32),
        pltpu.VMEM((rows, width), narrow),
        pltpu.VMEM((LOW, total // LOW * width), narrow),
        pltpu.VMEM((LOW, total // LOW * width), narrow),
        pltpu.VMEM((LOW, slots // LOW * width), jnp.float32),
        pltpu.SemaphoreType.DMA((2, LAYERS * (2 + 3 * PEERS))),
        pltpu.SemaphoreType.DMA((2, len(halves))),
    ]
    whole = pl.BlockSpec(memory_space=pltpu.VMEM)
    return pl.pallas_call(
        functools.partial(kernel, lax.axis_size("dom")),
        out_shape=(
            jax.ShapeDtypeStruct((node_total, width), narrow),
            jax.ShapeDtypeStruct((rows, width), narrow),
        ),
        in_specs=[pl.BlockSpec(memory_space=pltpu.SMEM)] + [whole] * 9,
        out_specs=(whole, whole),
        scratch_shapes=scratch,
        compiler_params=pltpu.CompilerParams(
            collective_id=0, has_side_effects=True, vmem_limit_bytes=48 * 1024 * 1024
        ),
    )(
        edge_count,
        node_latent,
        edge_latent,
        edge_sender.reshape(1, rows),
        edge_receiver.reshape(1, rows),
        index_row,
        *halves,
    )


def solution(mesh):
    return jax.shard_map(
        local,
        mesh=mesh,
        in_specs=(
            P("dom", None),
            P(("dom", "tp"), None),
            P(("dom", "tp")),
            P(("dom", "tp")),
            P(("dom", "tp")),
            P("dom", None, None),
            P(None, None, "tp"),
            P(None, "tp", None),
            P(None, None, "tp"),
            P(None, "tp", None),
        ),
        out_specs=(P("dom", None), P(("dom", "tp"), None)),
        check_vma=False,
    )
```

time: 331 us -> 71.5 us (0.22); the launches traced: 327 us -> 71.3 us
  matrix products: 176 us -> 0 us
  Pallas kernels: 0 us -> 65.1 us
  starting transfers between devices: 50.5 us -> 0 us
  waiting for transfers between devices: 35 us -> 0 us
  other arithmetic: 24.3 us -> 0 us
  blocking collectives: 13.7 us -> 0 us
  between operations: 14.8 us -> 1.37 us
  local copies, waits for them, and re-layouts: 11 us -> 4.91 us
    dot_general x132 -> x0, matrix products: 176 us -> none  [the longest x105 113 us: product(): jnp.dot(first_operand, second_operand, preferred_element_type=jnp.float32)]
    pallas_call x0 -> x1, Pallas kernels: none -> 65.1 us  [local(): pl.pallas_call(functools.partial(kernel, lax.axis_size('dom')), out_shape...]
    ppermute x24 -> x0, starting transfers between devices: 50.3 us -> none  [from_behind(): lax.ppermute(array, axis, [(i, (i + by) % length) for i in range(length)])]
    ppermute x24 -> x0, waiting for transfers between devices: 21.5 us -> none  [from_behind(): lax.ppermute(array, axis, [(i, (i + by) % length) for i in range(length)])]
    all_gather x7 -> x0, blocking collectives: 13.7 us -> none  [the longest x3 5.98 us: local(): nodes_now = lax.all_gather(renewed, 'tp', axis=0, tiled=True)]
    reduce_scatter x3 -> x0, waiting for transfers between devices: 13.5 us -> none  [local(): lax.psum_scatter(owned_sums, 'tp', scatter_dimension=0, tiled=True)]
    dynamic_update_slice x24 -> x0, other arithmetic: 8.68 us -> none  [local(): summed, renewed_blocks = lax.scan(edge_block, start_sums, edge_pieces)]
    convert_element_type x27 -> x0, other arithmetic: 6.71 us -> none  [the longest x24 6.56 us: edge_block(): message = jnp.where(live_mask[:, None], layer_norm(product(edge_hidden, w...]
  transfers between devices with their start and end apart: 27 -> 0, of which waited for: 11 -> 0; matrix products, arithmetic and copies ran while one was open for 1% -> 0% of each run, Pallas kernels for 0% -> 0%
where the time goes in v3:
time: 71.5 us; the launch traced here: 71.3 us
  Pallas kernels  65.1 us (91%)
  local copies, waits for them, and re-layouts  4.91 us (7%)
  between operations  1.37 us (2%)
    pallas_call x1, Pallas kernels, local(): pl.pallas_call(functools.partial(kernel, lax.axis_size('dom')), out_shape...  65.1 us
    unnamed x20, local copies, waits for them, and re-layouts  4.91 us

profile of v3, /device:TPU:0, one launch (start us, length us, event | category | flops | bytes accessed | tf_op | source)
XLA Modules:
  0.0 71.3 jit_solution(2804960537855983163)
XLA Ops:
  1.3 0.0 copy-start.7
  1.3 1.1 %copy.13.refs_8_ = bf16[3,256,64]{2,1,0:T(8,128)(2,1)S(1)} copy(bf16[3,256,64]{1,2,0:T(8,128)(2,1)} %param.18) | data formatting | bytes 196608 | tf_op args[8]
  2.4 0.0 copy-done.7
  2.4 0.0 copy-start.1
  2.4 0.0 copy-start.2
  2.4 0.0 copy-start.3
  2.4 0.0 copy-start.4
  2.4 0.0 copy-start.5
  2.5 0.0 copy-start.6
  2.5 0.2 copy.12.refs_6_
  2.7 0.7 copy-done.1
  3.3 0.0 copy-done.2
  3.3 0.0 copy-done.3
  3.3 0.0 copy-done.4
  3.4 0.0 copy-done.5
  3.4 0.0 copy-done.6
  3.4 0.0 copy-start
  3.4 1.2 %copy-done = bf16[4096,128]{1,0:T(8,128)(2,1)S(1)} copy-done((bf16[4096,128]{1,0:T(8,128)(2,1)S(1)}, bf16[4096,128]{1,0:T(8,128)(2,1)}, u32[]{:S(2)}) %copy-start) | copy-done | bytes 1048600
  4.6 65.1 %shard_map.113 = (bf16[1024,128]{1,0:T(8,128)(2,1)S(1)}, bf16[4096,128]{1,0:T(8,128)(2,1)S(1)}) custom-call(s32[1]{0:T(128)S(6)} %copy.16.refs_0_, bf16[1024,128]{1,0:T(8,128)(2,1)S(1)} %copy-done.1, bf16[4096,128]{1,0:T(8,128)(2,1)S(1)} %copy-done, s32[1,4096]{1,0:T(1,128)S(1)} %bitcast.3, s32[1,4096]{1,0:T(1,128)S(1)} %bitcast.4, s32[1,512]{1,0:T(1,128)S(1)} %bitcast.5, ...), custom_call_target="tpu_custom_call" | custom-call | tf_op jit(solution)/shard_map/pallas_call | solution.py:339
  69.7 0.7 copy.17
  70.4 1.0 %copy.18 = bf16[4096,128]{1,0:T(8,128)(2,1)} copy(bf16[4096,128]{1,0:T(8,128)(2,1)S(1)} %get-tuple-element.5) | data formatting | bytes 2097152
Async XLA Ops:
  1.3 1.1 %copy-start.7 = (bf16[3,384,64]{1,2,0:T(8,128)(2,1)S(1)}, bf16[3,384,64]{1,2,0:T(8,128)(2,1)}, u32[]{:S(2)}) copy-start(bf16[3,384,64]{1,2,0:T(8,128)(2,1)} %param.16) | copy-start | bytes 442372
  2.4 1.0 %copy-start.1 = (bf16[1024,128]{1,0:T(8,128)(2,1)S(1)}, bf16[1024,128]{1,0:T(8,128)(2,1)}, u32[]{:S(2)}) copy-start(bf16[1024,128]{1,0:T(8,128)(2,1)} %refs_1_.1) | copy-start | bytes 786436
  2.4 0.9 %copy-start.2 = (bf16[3,64,128]{2,1,0:T(8,128)(2,1)S(1)}, bf16[3,64,128]{2,1,0:T(8,128)(2,1)}, u32[]{:S(2)}) copy-start(bf16[3,64,128]{2,1,0:T(8,128)(2,1)} %refs_7_.1) | copy-start | bytes 147460
  2.4 0.9 %copy-start.3 = (bf16[3,64,128]{2,1,0:T(8,128)(2,1)S(1)}, bf16[3,64,128]{2,1,0:T(8,128)(2,1)}, u32[]{:S(2)}) copy-start(bf16[3,64,128]{2,1,0:T(8,128)(2,1)} %refs_9_.1) | copy-start | bytes 147460
  2.4 0.9 %copy-start.4 = (s32[4096]{0:T(1024)S(1)}, s32[4096]{0:T(1024)}, u32[]{:S(2)}) copy-start(s32[4096]{0:T(1024)} %param.12) | copy-start | bytes 49156
  2.4 0.9 %copy-start.5 = (s32[4096]{0:T(1024)S(1)}, s32[4096]{0:T(1024)}, u32[]{:S(2)}) copy-start(s32[4096]{0:T(1024)} %param.13) | copy-start | bytes 49156
  2.5 0.9 %copy-start.6 = (s32[1,4,128]{2,1,0:T(4,128)S(1)}, s32[1,4,128]{2,1,0:T(4,128)}, u32[]{:S(2)}) copy-start(s32[1,4,128]{2,1,0:T(4,128)} %param.15) | copy-start | bytes 6148
  3.4 1.2 %copy-start = (bf16[4096,128]{1,0:T(8,128)(2,1)S(1)}, bf16[4096,128]{1,0:T(8,128)(2,1)}, u32[]{:S(2)}) copy-start(bf16[4096,128]{1,0:T(8,128)(2,1)} %refs_2_.1) | copy-start | bytes 3145732

commit v4 on v3

--- a/solution.py
+++ b/solution.py
@@ -84,8 +84,26 @@
             full[layer, rows:, :] = jnp.where(mine == 0, far, near)
 
 
+def double_block(weight):
+    gap = jnp.zeros_like(weight)
+    top = jnp.concatenate([weight, gap], axis=1)
+    return jnp.concatenate([top, jnp.concatenate([gap, weight], axis=1)], axis=0)
+
+
+def paired_product(values, doubled):
+    rows, width = values.shape
+    pairs = jnp.concatenate([values[: rows // 2], values[rows // 2 :]], axis=1)
+    out = product(pairs, doubled)
+    return jnp.concatenate([out[:, :width], out[:, width:]], axis=0)
+
+
+def unit_spread(centred):
+    spread = jnp.mean(centred * centred, axis=-1, keepdims=True)
+    return centred * lax.rsqrt(spread + norm_floor)
+
+
 LOW = 256
-BLOCK = 1024
+BLOCK = 4096
 
 
 def kernel(size, *refs):
@@ -95,7 +113,7 @@
     others, fulls, refs = refs[2:6], refs[6:10], refs[10:]
     outgoing, halo_in, back_out, back_near, back_far, own_sums, own_far = refs[:7]
     pick, place, low_hot, tops, recv_hot, linear, messages = refs[7:14]
-    send_table, recv_table, back_sums, sems, weight_sems = refs[14:]
+    send_table, recv_table, back_sums, out_pair, sems, weight_sems = refs[14:]
     edge_in, edge_out, node_in, node_out = fulls
     node_total, width = nodes_ref.shape
     rows = edges_ref.shape[0]
@@ -190,6 +208,9 @@
         base = layer * per_layer
         more = layer + 1 < LAYERS
         latents = latent_ref if layer == 0 else edges_ref
+        second = edge_out[layer].astype(jnp.float32)
+        second = second - jnp.mean(second, axis=1, keepdims=True)
+        out_pair[layer] = double_block(second.astype(jnp.bfloat16))
         for h in range(own_high):
             fill_tables(layer, nodes_ref[h * LOW : (h + 1) * LOW, :], h)
 
@@ -211,7 +232,7 @@
             found = linear[here, :] + gathered(0, at, send_table, own_high, high)
             found = found + gathered(1, at, recv_table, own_high, high)
             hidden = jnp.maximum(found, 0.0).astype(jnp.bfloat16)
-            message = layer_norm(product(hidden, edge_out[layer]))
+            message = unit_spread(paired_product(hidden, out_pair[layer]))
             position = lax.broadcasted_iota(jnp.int32, (block, width), 0) + at
             message = jnp.where(position < count_ref[0], message, 0.0).astype(jnp.bfloat16)
             messages[here, :] = message
@@ -332,6 +353,7 @@
         pltpu.VMEM((LOW, total // LOW * width), narrow),
         pltpu.VMEM((LOW, total // LOW * width), narrow),
         pltpu.VMEM((LOW, slots // LOW * width), jnp.float32),
+        pltpu.VMEM((LAYERS, 2 * width, 2 * width), narrow),
         pltpu.SemaphoreType.DMA((2, LAYERS * (2 + 3 * PEERS))),
         pltpu.SemaphoreType.DMA((2, len(halves))),
     ]

time: 71.5 us -> 63.1 us (0.88)
  Pallas kernels: 65.1 us -> 56.6 us
    pallas_call x1, Pallas kernels: 65.1 us -> 56.6 us  [local(): pl.pallas_call(functools.partial(kernel, lax.axis_size('dom')), out_shape...]
where the time goes in v4:
time: 63.1 us; the launch traced here: 62.9 us
  Pallas kernels  56.6 us (90%)
  local copies, waits for them, and re-layouts  4.91 us (8%)
  between operations  1.37 us (2%)
    pallas_call x1, Pallas kernels, local(): pl.pallas_call(functools.partial(kernel, lax.axis_size('dom')), out_shape...  56.6 us
    unnamed x20, local copies, waits for them, and re-layouts  4.91 us

profile of v4, /device:TPU:0, one launch (start us, length us, event | category | flops | bytes accessed | tf_op | source)
XLA Modules:
  0.0 62.9 jit_solution(1245755902759905617)
XLA Ops:
  1.3 0.0 copy-start.7
  1.3 1.1 %copy.13.refs_8_ = bf16[3,256,64]{2,1,0:T(8,128)(2,1)S(1)} copy(bf16[3,256,64]{1,2,0:T(8,128)(2,1)} %param.18) | data formatting | bytes 196608 | tf_op args[8]
  2.4 0.0 copy-done.7
  2.4 0.0 copy-start.1
  2.4 0.0 copy-start.2
  2.4 0.0 copy-start.3
  2.4 0.0 copy-start.4
  2.4 0.0 copy-start.5
  2.5 0.0 copy-start.6
  2.5 0.2 copy.12.refs_6_
  2.7 0.7 %copy-done.1 = bf16[1024,128]{1,0:T(8,128)(2,1)S(1)} copy-done((bf16[1024,128]{1,0:T(8,128)(2,1)S(1)}, bf16[1024,128]{1,0:T(8,128)(2,1)}, u32[]{:S(2)}) %copy-start.1) | copy-done | bytes 262168
  3.3 0.0 copy-done.2
  3.3 0.0 copy-done.3
  3.3 0.0 copy-done.4
  3.4 0.0 copy-done.5
  3.4 0.0 copy-done.6
  3.4 0.0 copy-start
  3.4 1.2 %copy-done = bf16[4096,128]{1,0:T(8,128)(2,1)S(1)} copy-done((bf16[4096,128]{1,0:T(8,128)(2,1)S(1)}, bf16[4096,128]{1,0:T(8,128)(2,1)}, u32[]{:S(2)}) %copy-start) | copy-done | bytes 1048600
  4.6 56.6 %shard_map.113 = (bf16[1024,128]{1,0:T(8,128)(2,1)S(1)}, bf16[4096,128]{1,0:T(8,128)(2,1)S(1)}) custom-call(s32[1]{0:T(128)S(6)} %copy.16.refs_0_, bf16[1024,128]{1,0:T(8,128)(2,1)S(1)} %copy-done.1, bf16[4096,128]{1,0:T(8,128)(2,1)S(1)} %copy-done, s32[1,4096]{1,0:T(1,128)S(1)} %bitcast.3, s32[1,4096]{1,0:T(1,128)S(1)} %bitcast.4, s32[1,512]{1,0:T(1,128)S(1)} %bitcast.5, ...), custom_call_target="tpu_custom_call" | custom-call | tf_op jit(solution)/shard_map/pallas_call | solution.py:361
  61.2 0.7 %copy.17 = bf16[1024,128]{1,0:T(8,128)(2,1)} copy(bf16[1024,128]{1,0:T(8,128)(2,1)S(1)} %get-tuple-element.4) | data formatting | bytes 524288
  61.9 1.0 %copy.18 = bf16[4096,128]{1,0:T(8,128)(2,1)} copy(bf16[4096,128]{1,0:T(8,128)(2,1)S(1)} %get-tuple-element.5) | data formatting | bytes 2097152
Async XLA Ops:
  1.3 1.1 %copy-start.7 = (bf16[3,384,64]{1,2,0:T(8,128)(2,1)S(1)}, bf16[3,384,64]{1,2,0:T(8,128)(2,1)}, u32[]{:S(2)}) copy-start(bf16[3,384,64]{1,2,0:T(8,128)(2,1)} %param.16) | copy-start | bytes 442372
  2.4 1.0 %copy-start.1 = (bf16[1024,128]{1,0:T(8,128)(2,1)S(1)}, bf16[1024,128]{1,0:T(8,128)(2,1)}, u32[]{:S(2)}) copy-start(bf16[1024,128]{1,0:T(8,128)(2,1)} %refs_1_.1) | copy-start | bytes 786436
  2.4 0.9 %copy-start.2 = (bf16[3,64,128]{2,1,0:T(8,128)(2,1)S(1)}, bf16[3,64,128]{2,1,0:T(8,128)(2,1)}, u32[]{:S(2)}) copy-start(bf16[3,64,128]{2,1,0:T(8,128)(2,1)} %refs_7_.1) | copy-start | bytes 147460
  2.4 0.9 %copy-start.3 = (bf16[3,64,128]{2,1,0:T(8,128)(2,1)S(1)}, bf16[3,64,128]{2,1,0:T(8,128)(2,1)}, u32[]{:S(2)}) copy-start(bf16[3,64,128]{2,1,0:T(8,128)(2,1)} %refs_9_.1) | copy-start | bytes 147460
  2.4 0.9 %copy-start.4 = (s32[4096]{0:T(1024)S(1)}, s32[4096]{0:T(1024)}, u32[]{:S(2)}) copy-start(s32[4096]{0:T(1024)} %param.12) | copy-start | bytes 49156
  2.4 0.9 %copy-start.5 = (s32[4096]{0:T(1024)S(1)}, s32[4096]{0:T(1024)}, u32[]{:S(2)}) copy-start(s32[4096]{0:T(1024)} %param.13) | copy-start | bytes 49156
  2.5 0.9 %copy-start.6 = (s32[1,4,128]{2,1,0:T(4,128)S(1)}, s32[1,4,128]{2,1,0:T(4,128)}, u32[]{:S(2)}) copy-start(s32[1,4,128]{2,1,0:T(4,128)} %param.15) | copy-start | bytes 6148
  3.4 1.2 %copy-start = (bf16[4096,128]{1,0:T(8,128)(2,1)S(1)}, bf16[4096,128]{1,0:T(8,128)(2,1)}, u32[]{:S(2)}) copy-start(bf16[4096,128]{1,0:T(8,128)(2,1)} %refs_2_.1) | copy-start | bytes 3145732
